TPU v7x, 16 devices: a 4x2x1 block of a 4x4x8 slice. The times are simulated.
16 devices in a mesh: rep: 4 (over y, z, core), dp: 4 (over x).
Axes of the slice: x: 4, y: 2, z: 1, core: 2. Of those that a mesh axis runs over, the one named last changes fastest.
The devices are a block of a 4x4x8 slice.
Arguments:
- x: bfloat16 [16, 4096, 640], P(('rep', 'dp')), parts along dimension 0
- dy: bfloat16 [16, 4096, 640], P(('rep', 'dp')), parts along dimension 0
- w_gate: bfloat16 [2, 640, 1536], replicated
- w_up: bfloat16 [2, 640, 1536], replicated
- w_down: bfloat16 [2, 1536, 640], replicated
- m_w_gate: float32 [2, 640, 1536], P(None, 'dp')
- m_w_up: float32 [2, 640, 1536], P(None, 'dp')
- m_w_down: float32 [2, 1536, 640], P(None, 'dp')
- v_w_gate: float32 [2, 640, 1536], P(None, 'dp')
- v_w_up: float32 [2, 640, 1536], P(None, 'dp')
- v_w_down: float32 [2, 1536, 640], P(None, 'dp')
Outputs:
- output 1: bfloat16 [8, 640, 1536], P('rep'), parts along dimension 0
- output 2: bfloat16 [8, 640, 1536], P('rep'), parts along dimension 0
- output 3: bfloat16 [8, 1536, 640], P('rep'), parts along dimension 0
- output 4: float32 [8, 640, 1536], P('rep', 'dp'), parts along dimension 0
- output 5: float32 [8, 640, 1536], P('rep', 'dp'), parts along dimension 0
- output 6: float32 [8, 1536, 640], P('rep', 'dp'), parts along dimension 0
- output 7: float32 [8, 640, 1536], P('rep', 'dp'), parts along dimension 0
- output 8: float32 [8, 640, 1536], P('rep', 'dp'), parts along dimension 0
- output 9: float32 [8, 1536, 640], P('rep', 'dp'), parts along dimension 0
There are 4 independent parts. A program takes and returns all parts, laid end to end along the dimension named above; an argument that names none is the same for every part.
All inputs are finite; a program needn't handle non-finite values.
Results may differ from a plain program's by a relative error of at most 0.022.
Values are sent between devices in bfloat16 or wider.
A program may use at most 768 MiB of HBM per device.

v0:
```python
import jax
import jax.numpy as jnp
from jax import lax

NAMES = ("w_gate", "w_up", "w_down")


def matmul(a, w):
    return jnp.dot(a, w, preferred_element_type=jnp.float32).astype(jnp.bfloat16)


def normed(h):
    wide = h.astype(jnp.float32)
    scale = lax.rsqrt(jnp.mean(wide**2, -1, keepdims=True) + 1e-6)
    return (wide * scale).astype(jnp.bfloat16)


def layer(h, w):
    a = normed(h)
    gate = jnp.dot(a, w["w_gate"], preferred_element_type=jnp.float32)
    up = jnp.dot(a, w["w_up"], preferred_element_type=jnp.float32)
    return h + matmul((jax.nn.silu(gate) * up).astype(jnp.bfloat16), w["w_down"])


def adamw(w, m, v, g):
    m = 0.9 * m + 0.1 * g
    v = 0.95 * v + 0.05 * g * g
    step = m * lax.rsqrt(v + 1e-8) + 0.1 * w
    return (w - 0.02 * step).astype(jnp.bfloat16), m, v


def clipped(gradients, sum_of_squares, count):
    factor = jnp.minimum(1.0, 0.5 * lax.rsqrt(sum_of_squares / count + 1e-30))
    return [g * factor for g in gradients]


def stack(weights, h):
    for number in range(weights["w_gate"].shape[0]):
        h = layer(h, {name: w[number] for name, w in weights.items()})
    return h


def solution(mesh):
    groups = mesh.shape["rep"]

    def step(x, dy, *arrays):
        weights, m, v = (arrays[i : i + 3] for i in (0, 3, 6))
        x, dy = (t.reshape(groups, -1, *t.shape[1:]) for t in (x, dy))

        def of_a_group(x, dy):
            _, back = jax.vjp(lambda w: stack(w, x), dict(zip(NAMES, weights, strict=True)))
            by_weights = back(dy)[0]
            gradients = [by_weights[name].astype(jnp.float32) for name in NAMES]
            gradients = clipped(gradients, sum(jnp.sum(g * g) for g in gradients), sum(g.size for g in gradients))
            new = [adamw(w.astype(jnp.float32), m, v, g) for w, m, v, g in zip(weights, m, v, gradients, strict=True)]
            return tuple(one[which] for which in range(3) for one in new)

        return tuple(t.reshape(-1, *t.shape[2:]) for t in jax.vmap(of_a_group)(x, dy))

    return step
```

profile of v0, /device:TPU:112, one launch (start us, length us, event | category | flops | bytes accessed | tf_op | source)
XLA Modules:
  0.0 633.8 jit_solution(17934523325220189787)
XLA Ops:
  7.3 3.6 fusion.33
  10.9 8.1 %copy = bf16[1,4096,640]{1,2,0:T(8,128)(2,1)} copy(bf16[1,4096,640]{2,1,0:T(8,128)(2,1)} %param.2) | data formatting | bytes 10485760 | tf_op args[0]
  19.0 17.3 %fusion.83 = f32[4096,1536]{1,0:T(8,128)} fusion(bf16[1,4096,640]{2,1,0:T(8,128)(2,1)} %param.2, f32[4096]{0:T(1024)S(1)} %add_rsqrt_fusion, bf16[2,640,1536]{2,1,0:T(8,128)(2,1)} %param), kind=kOutput, calls=%fused_computation.98 | convolution fusion | flops 8060928000 | bytes 32391168 | tf_op jit(solution)/vmap(jvp())/dot_general | solution.py:20
  36.3 13.4 %fusion.81 = f32[4096,1536]{1,0:T(8,128)} fusion(bf16[1,4096,640]{2,1,0:T(8,128)(2,1)S(1)} %bitcast.323, f32[4096]{0:T(1024)S(1)} %add_rsqrt_fusion, bf16[2,640,1536]{2,1,0:T(8,128)(2,1)S(1)} %copy-done.5), kind=kOutput, calls=%fused_computation.97 | convolution fusion | flops 8060928000 | bytes 32391168 | tf_op jit(solution)/vmap(jvp())/dot_general | solution.py:21
  49.7 21.8 %fusion.28 = bf16[4096,1536]{1,0:T(8,128)(2,1)} fusion(f32[4096,1536]{1,0:T(8,128)} %fusion.81, f32[4096,1536]{1,0:T(8,128)} %fusion.83), kind=kLoop, calls=%fused_computation.46 | loop fusion | flops 37748736 | bytes 62914560
  71.5 13.3 %fusion.37 = (f32[4096]{0:T(1024)S(1)}, bf16[1,1,4096,640]{2,3,1,0:T(8,128)(2,1)S(1)}) fusion(bf16[4096,1536]{1,0:T(8,128)(2,1)} %fusion.28, bf16[2,1536,640]{2,1,0:T(8,128)(2,1)S(1)} %copy-done.4, bf16[1,4096,640]{1,2,0:T(8,128)(2,1)} %copy), kind=kOutput, calls=%fused_computation.54 | convolution fusion | flops 8066166784 | bytes 25051136 | tf_op jit(solution)/vmap(jvp())/dot_general | solution.py:9
  84.9 0.6 copy-done.7
  85.5 16.1 %fusion.73 = f32[4096,1536]{1,0:T(8,128)} fusion(bf16[1,1,4096,640]{2,3,1,0:T(8,128)(2,1)S(1)} %get-tuple-element.10, f32[4096]{0:T(1024)S(1)} %bitcast.330, bf16[2,640,1536]{2,1,0:T(8,128)(2,1)} %param), kind=kOutput, calls=%fused_computation.77 | convolution fusion | flops 8060928000 | bytes 32391168 | tf_op jit(solution)/vmap(jvp())/dot_general | solution.py:20
  101.6 13.5 %fusion.75 = f32[4096,1536]{1,0:T(8,128)} fusion(bf16[1,1,4096,640]{2,3,1,0:T(8,128)(2,1)S(1)} %get-tuple-element.10, f32[4096]{0:T(1024)S(1)} %bitcast.331, bf16[2,640,1536]{2,1,0:T(8,128)(2,1)S(1)} %copy-done.6), kind=kOutput, calls=%fused_computation.78 | convolution fusion | flops 8060928000 | bytes 32391168 | tf_op jit(solution)/vmap(jvp())/dot_general | solution.py:21
  115.1 23.0 %fusion.59 = f32[1,1536,640]{2,1,0:T(8,128)} fusion(bf16[1,4096,640]{2,1,0:T(8,128)(2,1)} %param.5, f32[4096,1536]{1,0:T(8,128)} %fusion.75, f32[4096,1536]{1,0:T(8,128)} %fusion.73), kind=kOutput, calls=%fused_computation.74 | convolution fusion | flops 8090812416 | bytes 59506688 | tf_op jit(solution)/vmap(transpose(jvp()))/dot_general | solution.py:9
  138.2 13.3 %fusion.26 = bf16[1,1,4096,1536]{3,2,1,0:T(8,128)(2,1)S(1)} fusion(bf16[1,4096,640]{2,1,0:T(8,128)(2,1)} %param.5, bf16[2,1536,640]{2,1,0:T(8,128)(2,1)} %param.4), kind=kOutput, calls=%fused_computation.44 | convolution fusion | flops 8059355136 | bytes 19791872 | tf_op jit(solution)/vmap(transpose(jvp()))/dot_general | solution.py:9
  151.5 4.5 copy-done
  156.0 22.6 %fusion.6 = bf16[4096,1536]{1,0:T(8,128)(2,1)} fusion(f32[4096,1536]{1,0:T(8,128)} %fusion.73, f32[4096,1536]{1,0:T(8,128)} %fusion.75, bf16[1,1,4096,1536]{3,2,1,0:T(8,128)(2,1)S(1)} %fusion.26), kind=kLoop, calls=%fused_computation.11 | loop fusion | flops 75497472 | bytes 75497472
  178.6 18.2 %fusion.40 = bf16[4096,640]{0,1:T(8,128)(2,1)} fusion(bf16[1,1,4096,1536]{3,2,1,0:T(8,128)(2,1)} %copy-done, f32[4096,1536]{1,0:T(8,128)} %fusion.73, bf16[2,640,1536]{2,1,0:T(8,128)(2,1)} %param.3), kind=kOutput, calls=%fused_computation.60 | convolution fusion | flops 8093433856 | bytes 44957696 | tf_op jit(solution)/vmap(transpose(jvp()))/dot_general | solution.py:21
  196.8 7.9 %copy.1 = bf16[1,4096,640]{1,2,0:T(8,128)(2,1)} copy(bf16[1,4096,640]{2,1,0:T(8,128)(2,1)} %param.5) | data formatting | bytes 10485760 | tf_op args[1]
  204.7 18.2 %fusion.39 = (f32[4096]{0:T(1024)S(1)}, bf16[4096,640]{0,1:T(8,128)(2,1)}) fusion(bf16[1,1,4096,640]{2,3,1,0:T(8,128)(2,1)} %copy-done.1, bf16[4096,640]{0,1:T(8,128)(2,1)} %fusion.40, bf16[4096,1536]{1,0:T(8,128)(2,1)} %fusion.6, bf16[2,640,1536]{2,1,0:T(8,128)(2,1)} %param), kind=kOutput, calls=%fused_computation.56 | convolution fusion | flops 8066166784 | bytes 30294016 | tf_op jit(solution)/vmap(transpose(jvp()))/dot_general | solution.py:20
  223.0 12.0 %fusion.47 = bf16[4096,640]{0,1:T(8,128)(2,1)} fusion(bf16[1,1,4096,640]{2,3,1,0:T(8,128)(2,1)} %copy-done.1, bf16[4096,640]{0,1:T(8,128)(2,1)} %get-tuple-element.12, bf16[1,4096,640]{1,2,0:T(8,128)(2,1)} %copy.1, f32[4096]{0:T(1024)S(1)} %bitcast.329, f32[4096]{0:T(1024)S(1)} %bitcast.332), kind=kLoop, calls=%fused_computation.65 | loop fusion | flops 18350080 | bytes 21004288
  235.0 15.8 %convolution_bitcast_fusion = f32[1,1536,640]{2,1,0:T(8,128)} fusion(bf16[4096,1536]{1,0:T(8,128)(2,1)} %fusion.28, bf16[4096,640]{0,1:T(8,128)(2,1)} %fusion.47), kind=kOutput, calls=%fused_computation.72 | convolution fusion | flops 8053063680 | bytes 21757952 | tf_op jit(solution)/vmap(transpose(jvp()))/dot_general | solution.py:9
  250.9 20.1 %fusion.64 = f32[1,640,1536]{2,1,0:T(8,128)} fusion(bf16[1,1,4096,1536]{3,2,1,0:T(8,128)(2,1)} %copy-done, f32[4096,1536]{1,0:T(8,128)} %fusion.73, bf16[1,1,4096,640]{2,3,1,0:T(8,128)(2,1)} %copy-done.1, f32[4096]{0:T(1024)S(1)} %bitcast.333), kind=kOutput, calls=%fused_computation.75 | convolution fusion | flops 8098676736 | bytes 46940160 | tf_op jit(solution)/vmap(transpose(jvp()))/dot_general | solution.py:21
  271.1 15.9 %fusion.27 = bf16[1,1,4096,1536]{3,2,1,0:T(8,128)(2,1)} fusion(bf16[4096,640]{0,1:T(8,128)(2,1)} %fusion.47, bf16[2,1536,640]{2,1,0:T(8,128)(2,1)} %param.4), kind=kOutput, calls=%fused_computation.45 | convolution fusion | flops 8059355136 | bytes 19791872 | tf_op jit(solution)/vmap(transpose(jvp()))/dot_general | solution.py:9
  287.1 19.5 %fusion.67 = f32[1,640,1536]{2,1,0:T(8,128)} fusion(bf16[1,1,4096,1536]{3,2,1,0:T(8,128)(2,1)} %fusion.27, f32[4096,1536]{1,0:T(8,128)} %fusion.83, bf16[1,4096,640]{1,2,0:T(8,128)(2,1)} %copy, f32[4096]{0:T(1024)S(1)} %copy-done.12), kind=kOutput, calls=%fused_computation.76 | convolution fusion | flops 8098676736 | bytes 46940160 | tf_op jit(solution)/vmap(transpose(jvp()))/dot_general | solution.py:21
  306.7 14.3 %convolution_bitcast_fusion.1 = f32[1,640,1536]{2,1,0:T(8,128)} fusion(bf16[4096,1536]{1,0:T(8,128)(2,1)} %fusion.6, bf16[1,1,4096,640]{2,3,1,0:T(8,128)(2,1)} %copy-done.1, f32[4096]{0:T(1024)S(1)} %bitcast.334), kind=kOutput, calls=%fused_computation.73 | convolution fusion | flops 8060928000 | bytes 21774336 | tf_op jit(solution)/vmap(transpose(jvp()))/dot_general | solution.py:20
  321.1 29.9 %fusion.54 = f32[1,640,1536]{2,1,0:T(8,128)} fusion(f32[4096,1536]{1,0:T(8,128)} %fusion.83, f32[4096,1536]{1,0:T(8,128)} %fusion.81, bf16[1,1,4096,1536]{3,2,1,0:T(8,128)(2,1)} %fusion.27, bf16[1,4096,640]{1,2,0:T(8,128)(2,1)} %copy, f32[4096]{0:T(1024)S(1)} %copy-done.12), kind=kOutput, calls=%fused_computation.71 | convolution fusion | flops 8130134016 | bytes 72105984 | tf_op jit(solution)/vmap(transpose(jvp()))/dot_general | solution.py:20
  351.1 0.6 dynamic-slice
  352.4 1.3 convert_bitcast_fusion.4
  353.7 1.3 convert_bitcast_fusion.3
  354.9 1.1 fusion.95
  356.0 1.3 convert_bitcast_fusion.6
  357.3 23.0 %reduce-scatter.25.cloned.1.call-done = f32[1,160,1536]{2,1,0:T(8,128)} async-done(((f32[1,640,1536]{2,1,0:T(8,128)}), f32[1,160,1536]{2,1,0:T(8,128)}) %reduce-scatter.25.cloned.1.call-update) | async-done | bytes 983056
  380.3 1.3 convert_bitcast_fusion.5
  381.6 1.1 fusion.94
  382.7 40.7 %reduce-scatter.19.cloned.1.call-done = f32[1,160,1536]{2,1,0:T(8,128)} async-done(((f32[1,640,1536]{2,1,0:T(8,128)}), f32[1,160,1536]{2,1,0:T(8,128)}) %reduce-scatter.19.cloned.1.call-update) | async-done | bytes 983056
  423.4 1.3 convert_bitcast_fusion.8
  424.6 41.8 %reduce-scatter.21.cloned.1.call-done = f32[1,160,1536]{2,1,0:T(8,128)} async-done(((f32[1,640,1536]{2,1,0:T(8,128)}), f32[1,160,1536]{2,1,0:T(8,128)}) %reduce-scatter.21.cloned.1.call-update) | async-done | bytes 983056
  466.5 1.3 convert_bitcast_fusion.7
  467.7 1.1 fusion.93
  470.8 9.7 %all-reduce.16 = f32[1]{0:T(128)} all-reduce(f32[1]{0:T(128)} %bitcast.50), channel_id=5, replica_groups=mesh['rep'=4,'dp'=4] {'dp'}, use_global_device_ids=true, to_apply=%region_3.4.clone | all-reduce | flops 1 | bytes 8 | tf_op jit(solution)/vmap()/reduce_sum | solution.py:54
  481.2 5.8 fusion.130
  487.0 0.3 all-gather.10.cloned.1.call-start
  487.3 5.7 fusion.132
  493.2 5.8 fusion.131
  499.0 29.3 %all-gather.14.cloned.1.call-done = bf16[1,2,1536,640]{3,2,1,0:T(8,128)(2,1)} async-done(((bf16[1,2,384,640]{3,2,1,0:T(8,128)(2,1)}), bf16[1,2,1536,640]{3,2,1,0:T(8,128)(2,1)}) %all-gather.14.cloned.1.call-update) | async-done | bytes 3932176 | tf_op jit(solution)/reshape | solution.py:58
  528.3 44.3 %all-gather.10.cloned.1.call-done = bf16[1,2,640,1536]{3,2,1,0:T(8,128)(2,1)} async-done(((bf16[1,2,160,1536]{3,2,1,0:T(8,128)(2,1)}), bf16[1,2,640,1536]{3,2,1,0:T(8,128)(2,1)}) %all-gather.10.cloned.1.call-update) | async-done | bytes 3932176 | tf_op jit(solution)/reshape | solution.py:58
  572.6 44.3 %all-gather.12.cloned.1.call-done = bf16[1,2,640,1536]{3,2,1,0:T(8,128)(2,1)} async-done(((bf16[1,2,160,1536]{3,2,1,0:T(8,128)(2,1)}), bf16[1,2,640,1536]{3,2,1,0:T(8,128)(2,1)}) %all-gather.12.cloned.1.call-update) | async-done | bytes 3932176 | tf_op jit(solution)/reshape | solution.py:58
  616.9 4.5 copy.5
  621.4 2.0 copy.6
  623.4 1.5 copy-done.2
  624.9 1.9 copy.7
  (54 shorter events, 1.2 us)
Async XLA Ops:
  7.2 345.2 %reduce-scatter.27.cloned.1.call-start = ((), (), s32[]{:S(2)}) async-start(), calls=%async_computation.13 | async-start | bytes 4915200
  10.8 25.4 %slice-start = ((s8[5242880]{0:T(1024)(128)(4,1)}), s8[1048576]{0:T(1024)(128)(4,1)S(1)}, s32[]{:S(2)}) async-start(s8[5242880]{0:T(1024)(128)(4,1)} %bitcast.322), calls=%async_computation.15 | async-start | bytes 2097152
  19.0 17.3 %copy-start.11 = (f32[4096]{0:T(1024)}, f32[4096]{0:T(1024)S(1)}, u32[]{:S(2)}) copy-start(f32[4096]{0:T(1024)S(1)} %add_rsqrt_fusion) | copy-start | bytes 49156
  19.0 17.3 %slice-start.1 = ((s8[5242880]{0:T(1024)(128)(4,1)}), s8[4194304]{0:T(1024)(128)(4,1)S(1)}, s32[]{:S(2)}) async-start(s8[5242880]{0:T(1024)(128)(4,1)} %bitcast.322), calls=%async_computation.16 | async-start | bytes 8388608
  19.0 17.3 %copy-start.5 = (bf16[2,640,1536]{2,1,0:T(8,128)(2,1)S(1)}, bf16[2,640,1536]{2,1,0:T(8,128)(2,1)}, u32[]{:S(2)}) copy-start(bf16[2,640,1536]{2,1,0:T(8,128)(2,1)} %param.3) | copy-start | bytes 11796484
  49.7 21.8 %copy-start.4 = (bf16[2,1536,640]{2,1,0:T(8,128)(2,1)S(1)}, bf16[2,1536,640]{2,1,0:T(8,128)(2,1)}, u32[]{:S(2)}) copy-start(bf16[2,1536,640]{2,1,0:T(8,128)(2,1)} %param.4) | copy-start | bytes 11796484
  84.8 16.8 %copy-start.1 = (bf16[1,1,4096,640]{2,3,1,0:T(8,128)(2,1)}, bf16[1,1,4096,640]{2,3,1,0:T(8,128)(2,1)S(1)}, u32[]{:S(2)}) copy-start(bf16[1,1,4096,640]{2,3,1,0:T(8,128)(2,1)S(1)} %get-tuple-element.10) | copy-start | bytes 15728644
  84.9 0.7 copy-start.7
  84.9 16.7 %copy-start.9 = (f32[1,1,4096]{2,1,0:T(1,128)}, f32[1,1,4096]{2,1,0:T(1,128)S(1)}, u32[]{:S(2)}) copy-start(f32[1,1,4096]{2,1,0:T(1,128)S(1)} %rsqrt.38) | copy-start | bytes 49156
  85.5 16.1 %copy-start.6 = (bf16[2,640,1536]{2,1,0:T(8,128)(2,1)S(1)}, bf16[2,640,1536]{2,1,0:T(8,128)(2,1)}, u32[]{:S(2)}) copy-start(bf16[2,640,1536]{2,1,0:T(8,128)(2,1)} %param.3) | copy-start | bytes 11796484
  138.2 215.5 %reduce-scatter.29.cloned.1.call-start = ((), (), s32[]{:S(2)}) async-start(), calls=%async_computation.14 | async-start | bytes 4915200
  151.5 4.5 copy-start
  204.7 18.3 %copy-start.8 = (f32[4096]{0:T(1024)S(1)}, f32[4096]{0:T(1024)}, u32[]{:S(2)}) copy-start(f32[4096]{0:T(1024)} %copy-done.7) | copy-start | bytes 49156
  204.7 18.3 %copy-start.10 = (f32[1,1,4096]{2,1,0:T(1,128)S(1)}, f32[1,1,4096]{2,1,0:T(1,128)}, u32[]{:S(2)}) copy-start(f32[1,1,4096]{2,1,0:T(1,128)} %copy-done.9) | copy-start | bytes 49156
  250.9 105.2 %reduce-scatter.23.cloned.1.call-start = ((), (), s32[]{:S(2)}) async-start(), calls=%async_computation.11 | async-start | bytes 4915200
  271.1 16.0 %copy-start.12 = (f32[4096]{0:T(1024)S(1)}, f32[4096]{0:T(1024)}, u32[]{:S(2)}) copy-start(f32[4096]{0:T(1024)} %copy-done.11) | copy-start | bytes 49156
  271.1 109.2 %reduce-scatter.25.cloned.1.call-start = ((), (), s32[]{:S(2)}) async-start(), calls=%async_computation.12 | async-start | bytes 4915200
  306.6 116.8 %reduce-scatter.19.cloned.1.call-start = ((), (), s32[]{:S(2)}) async-start(), calls=%async_computation.9 | async-start | bytes 4915200
  321.0 30.1 %copy-start.13 = (u32[16]{0:T(128)S(1)}, u32[16]{0:T(128)}, u32[]{:S(2)}) copy-start(u32[16]{0:T(128)} %constant.74) | copy-start | bytes 196
  321.0 145.4 %reduce-scatter.21.cloned.1.call-start = ((), (), s32[]{:S(2)}) async-start(), calls=%async_computation.10 | async-start | bytes 4915200
  351.0 177.3 %all-gather.14.cloned.1.call-start = ((), (), s32[]{:S(2)}) async-start(), calls=%async_computation.8 | async-start | bytes 4915200 | tf_op jit(solution)/reshape | solution.py:58
  487.0 85.6 %all-gather.10.cloned.1.call-start = ((), (), s32[]{:S(2)}) async-start(), calls=%async_computation.6 | async-start | bytes 4915200 | tf_op jit(solution)/reshape | solution.py:58
  493.1 123.8 %all-gather.12.cloned.1.call-start = ((), (), s32[]{:S(2)}) async-start(), calls=%async_computation.7 | async-start | bytes 4915200 | tf_op jit(solution)/reshape | solution.py:58
  616.9 4.5 copy-start.3
  621.4 3.5 copy-start.2
Sparse Core Ops, SparseCore 0:
  138.3 43.5 reduce-scatter.26
  251.0 43.5 reduce-scatter.28
  296.8 40.3 reduce-scatter.22
  339.9 40.3 reduce-scatter.24
  383.0 40.3 reduce-scatter.18
  426.1 40.3 reduce-scatter.20
  487.1 41.1 all-gather.13
  530.5 42.1 all-gather.9
  574.7 42.1 all-gather.11
where the time goes:
time: 644 us; the launch traced here: 634 us
  matrix products  262 us (41%)
  waiting for transfers between devices  224 us (35%)
  other arithmetic  88.2 us (14%)
  local copies, waits for them, and re-layouts  31.6 us (5%)
  between operations  17.8 us (3%)
  blocking collectives  9.69 us (2%)
    reshape x3, waiting for transfers between devices, step(): t.reshape(-1, *t.shape[2:])  118 us
    unnamed x15, waiting for transfers between devices  106 us
    dot_general x5, matrix products, layer(): gate = jnp.dot(a, w['w_gate'], preferred_element_type=jnp.float32)  95.7 us
    dot_general x5, matrix products, layer(): up = jnp.dot(a, w['w_up'], preferred_element_type=jnp.float32)  84.7 us
    dot_general x5, matrix products, matmul(): jnp.dot(a, w, preferred_element_type=jnp.float32).astype(jnp.bfloat16)  81.2 us
    unnamed x4, other arithmetic  56.5 us
    unnamed x37, local copies, waits for them, and re-layouts  31 us
    reshape x3, other arithmetic, step(): t.reshape(-1, *t.shape[2:])  17.3 us
  transfers between devices with their start and end apart: 9, of which 6 were waited for; matrix products, arithmetic and copies ran while one was open for 36% of the time, Pallas kernels for 0%

commit v1 on v0

v1 whole, which is shorter than its diff:
```python
import functools

import jax
import jax.numpy as jnp
from jax import lax
from jax.experimental import pallas as pl
from jax.experimental.pallas import tpu as pltpu
from jax.sharding import PartitionSpec as P

F32, BF16 = jnp.float32, jnp.bfloat16
LANES = 128
AXIS = "dp"
MESH = pl.DeviceIdType.MESH
VMEM_LIMIT = 64000 * 1024
ROWS, COLS = (((0,), (0,)), ((), ())), (((1,), (1,)), ((), ()))


def dot(a, b):
    return jnp.dot(a, b, preferred_element_type=F32)


def dot_t(a, b):
    return lax.dot_general(a, b, COLS, preferred_element_type=F32)


def sigmoid(g):
    return 0.5 * jnp.tanh(0.5 * g) + 0.5


def normed(wide, axis):
    scale = lax.rsqrt(jnp.mean(wide * wide, axis, keepdims=True) + 1e-6)
    return (wide * scale).astype(BF16)


def forward_kernel(x_ref, dy_ref, wg_ref, wu_ref, wd_ref, a1_ref, a1t_ref, a2_ref, a2t_ref, h1t_ref, dyt_ref):
    ff = wg_ref.shape[1]
    part = 512
    dyt_ref[...] = dy_ref[...].T
    x = x_ref[...].astype(F32)
    a1 = normed(x, -1)
    a1_ref[...] = a1
    a1t_ref[...] = a1.T
    down = None
    for f in range(0, ff, part):
        gate = dot(a1, wg_ref[:, f : f + part])
        up = dot(a1, wu_ref[:, f : f + part])
        hidden = (gate * sigmoid(gate) * up).astype(BF16)
        term = dot(hidden, wd_ref[f : f + part, :])
        down = term if down is None else down + term
    h1 = (x + down.astype(BF16).astype(F32)).astype(BF16)
    h1t_ref[...] = h1.T
    a2 = normed(h1.astype(F32), -1)
    a2_ref[...] = a2
    a2t_ref[...] = a2.T


def forward(x, dy, wg, wu, wd, layer, tile=512):
    tokens, d = x.shape
    ff = wg.shape[-1]
    rows = pl.BlockSpec((tile, d), lambda t: (t, 0))
    columns = pl.BlockSpec((d, tile), lambda t: (0, t))
    weight = lambda a, b: pl.BlockSpec((None, a, b), lambda t: (layer, 0, 0))
    straight, turned = jax.ShapeDtypeStruct((tokens, d), BF16), jax.ShapeDtypeStruct((d, tokens), BF16)
    return pl.pallas_call(
        forward_kernel,
        grid=(tokens // tile,),
        in_specs=[rows, rows, weight(d, ff), weight(d, ff), weight(ff, d)],
        out_specs=[rows, columns, rows, columns, columns, columns],
        out_shape=[straight, turned, straight, turned, turned, turned],
        compiler_params=pltpu.CompilerParams(vmem_limit_bytes=VMEM_LIMIT),
        name="forward",
    )(x, dy, wg, wu, wd)


class Ring:
    def __init__(self, n, recv, summed, send_sem, recv_sem):
        self.me = lax.axis_index(AXIS)
        self.n, self.recv, self.summed, self.send_sem, self.recv_sem = n, recv, summed, send_sem, recv_sem
        self.right, self.left = (self.me + 1) % n, (self.me + n - 1) % n

    def copy(self, i, k, src, to):
        return pltpu.make_async_remote_copy(
            src_ref=src,
            dst_ref=self.recv.at[i, k],
            send_sem=self.send_sem.at[i, k],
            recv_sem=self.recv_sem.at[i, k],
            device_id={AXIS: to},
            device_id_type=MESH,
        )

    def hop(self, i, k, blocks):
        far = (self.me + 2) % self.n
        return self.copy(
            i,
            k,
            [
                lambda: blocks.at[far, 0],
                lambda: blocks.at[far, 1],
                lambda: blocks.at[self.right, 1],
                lambda: blocks.at[self.left, 0],
                lambda: self.summed.at[i, 0],
                lambda: self.summed.at[i, 1],
            ][k](),
            (self.right, self.left)[k % 2],
        )

    def start(self, i, blocks):
        for k in range(4):
            self.hop(i, k, blocks).start()

    def pass_on(self, i, blocks):
        for k, to in enumerate((self.right, self.left)):
            self.hop(i, k, blocks).wait_recv()
            self.summed[i, k] = (blocks[to, k].astype(F32) + self.recv[i, k].astype(F32)).astype(BF16)
            self.hop(i, 4 + k, blocks).start()

    def finish(self, i, blocks):
        for k in range(6):
            hop = self.hop(i, k, blocks)
            if k >= 2:
                hop.wait_recv()
            hop.wait_send()
        me = self.me
        return [
            (blocks[me, half].astype(F32) + self.recv[i, 4 + half].astype(F32) + self.recv[i, 3 - half].astype(F32)).astype(BF16)
            for half in range(2)
        ]


def pack(blocks, n, acc_g, acc_u, acc_d):
    d = acc_g.shape[0]
    half = d // n // 2
    for o in range(n):
        for h in range(2):
            rows = slice((2 * o + h) * half, (2 * o + h + 1) * half)
            blocks[o, h, 0:half, :] = acc_g[rows, :].astype(BF16)
            blocks[o, h, half : 2 * half, :] = acc_u[rows, :].astype(BF16)
            for b in range(n):
                blocks[o, h, 2 * half : 3 * half, b * LANES : (b + 1) * LANES] = acc_d[
                    (h * n + b) * half : (h * n + b + 1) * half, o * LANES : (o + 1) * LANES
                ].astype(BF16)


def unpack(halves, n, gu_ref, d_ref, ss_ref):
    half = halves[0].shape[0] // 3
    squares = jnp.zeros(ss_ref.shape, F32)
    for h, block in enumerate(halves):
        gu_ref[0, h * half : (h + 1) * half, :] = block[0:half]
        gu_ref[1, h * half : (h + 1) * half, :] = block[half : 2 * half]
        wide = block.astype(F32)
        s = jnp.sum((wide * wide).reshape(-1, 8, wide.shape[1]), axis=0)
        for b in range(n):
            squares = squares + s[:, b * LANES : (b + 1) * LANES]
            d_ref[:, (h * n + b) * half : (h * n + b + 1) * half] = block[2 * half :, b * LANES : (b + 1) * LANES].astype(F32).T.astype(BF16)
    ss_ref[...] = squares


def greet(peers):
    barrier = pltpu.get_barrier_semaphore()
    for peer in peers:
        pl.semaphore_signal(barrier, inc=1, device_id={AXIS: peer}, device_id_type=MESH)
    pl.semaphore_wait(barrier, len(peers))


def backward_kernel(n, chunks, tiles, carried, inner, *refs):
    refs = list(refs)
    take = lambda count: [refs.pop(0) for _ in range(count)]
    a_ref, at_ref, dy_ref, dyt_ref, wg_ref, wu_ref, wd_ref = take(7)
    h1t_ref = take(1)[0] if inner else None
    carried_ref = take(1)[0] if carried else None
    done = chunks - 1 + carried
    outs = [take(3) for _ in range(done)]
    last_ref = take(1)[0]
    dh_ref, dht_ref = take(2) if inner else (None, None)
    acc_g, acc_u, acc_d, blocks, recv, summed, send_sem, recv_sem = take(8)
    dat_ref = take(1)[0] if inner else None

    c, t = pl.program_id(0), pl.program_id(1)
    tile = a_ref.shape[0]
    own = wg_ref.shape[1] // n
    ring = Ring(n, recv, summed, send_sem, recv_sem)

    @pl.when((c == 0) & (t == 0))
    def _():
        greet((ring.left, ring.right))
        if carried:
            ring.start(0, carried_ref)

    places = [pl.ds(pl.multiple_of(o * own + c * LANES, LANES), LANES) for o in range(n)]
    wg = jnp.concatenate([wg_ref[:, p] for p in places], axis=1)
    wu = jnp.concatenate([wu_ref[:, p] for p in places], axis=1)
    wd = jnp.concatenate([wd_ref[p, :] for p in places], axis=0)

    a, dy = a_ref[...], dy_ref[...]
    gate, up = dot(a, wg), dot(a, wu)
    dhidden = dot_t(dy, wd).astype(BF16).astype(F32)
    s = sigmoid(gate)
    silu = gate * s
    hidden = (silu * up).astype(BF16)
    dup = (dhidden * silu).astype(BF16)
    dgate = (dhidden * up * (s + silu * (1 - s))).astype(BF16)
    at, dyt = at_ref[...], dyt_ref[...]
    accs = acc_g, acc_u, acc_d

    @pl.when(t == 0)
    def _():
        for acc in accs:
            acc[...] = jnp.zeros_like(acc)

    acc_g[...] += dot(at, dgate)
    acc_u[...] += dot(at, dup)
    acc_d[...] += dot(dyt, hidden)

    if inner:
        here = pl.ds(pl.multiple_of(t * tile, tile), tile)

        @pl.when(c == 0)
        def _():
            dat_ref[:, here] = jnp.zeros((dat_ref.shape[0], tile), F32)

        dat_ref[:, here] += dot_t(wg, dgate) + dot_t(wu, dup)

        @pl.when(c == chunks - 1)
        def _():
            da = dat_ref[:, here].astype(BF16).astype(F32)
            wide = h1t_ref[...].astype(F32)
            scale = lax.rsqrt(jnp.mean(wide * wide, 0, keepdims=True) + 1e-6)
            along = jnp.mean(da * wide, 0, keepdims=True)
            dwide = da * scale - wide * (scale * scale * scale * along)
            dht = (dyt.astype(F32) + dwide.astype(BF16).astype(F32)).astype(BF16)
            dht_ref[...] = dht
            dh_ref[...] = dht.T

    for step in range(chunks):
        i = step - 1 + carried
        if i < 0:
            continue
        source = carried_ref if carried and i == 0 else blocks.at[i - carried]

        @pl.when((c == step) & (t == tiles // 2 - 1))
        def _():
            ring.pass_on(i, source)

        @pl.when((c == step) & (t == tiles - 1))
        def _():
            unpack(ring.finish(i, source), n, *outs[i])

    for step in range(chunks - 1):

        @pl.when((c == step) & (t == tiles - 1))
        def _():
            pack(blocks.at[step], n, *accs)
            ring.start(step + carried, blocks.at[step])

    @pl.when((c == chunks - 1) & (t == tiles - 1))
    def _():
        pack(last_ref, n, *accs)


def backward(n, a, at, dy, dyt, wg, wu, wd, layer, h1t=None, carried=None, tile=1024, collective_id=0):
    tokens, d = a.shape
    ff = wg.shape[-1]
    chunks = ff // n // LANES
    tiles = tokens // tile
    inner, carry = h1t is not None, int(carried is not None)
    width, rows = n * LANES, 3 * (d // n // 2)
    done = chunks - 1 + carry
    straight = pl.BlockSpec((tile, d), lambda c, t: (t, 0))
    turned = pl.BlockSpec((d, tile), lambda c, t: (0, t))
    weight = lambda a, b: pl.BlockSpec((None, a, b), lambda c, t: (layer, 0, 0), pipeline_mode=pl.Buffered(1))
    whole = lambda *shape: pl.BlockSpec(shape, lambda c, t: (0,) * len(shape))
    once = lambda *shape: pl.BlockSpec(shape, lambda c, t: (0,) * len(shape), pipeline_mode=pl.Buffered(1))
    at_last = lambda c, t: jnp.where(c == chunks - 1, t, 0)
    packed = (n, 2, rows, width)
    in_specs = [straight, turned, straight, turned, weight(d, ff), weight(d, ff), weight(ff, d)]
    args = [a, at, dy, dyt, wg, wu, wd]
    if inner:
        in_specs.append(pl.BlockSpec((d, tile), lambda c, t: (0, at_last(c, t))))
        args.append(h1t)
    if carry:
        in_specs.append(once(*packed))
        args.append(carried)
    out_specs, out_shape = [], []
    for _ in range(done):
        for shape, dtype in (((2, d // n, width), BF16), ((LANES, d), BF16), ((8, LANES), F32)):
            out_specs.append(whole(*shape))
            out_shape.append(jax.ShapeDtypeStruct(shape, dtype))
    out_specs.append(whole(*packed))
    out_shape.append(jax.ShapeDtypeStruct(packed, BF16))
    scratch = [pltpu.VMEM((d, width), F32)] * 3 + [
        pltpu.VMEM((chunks - 1, *packed), BF16),
        pltpu.VMEM((done, 6, rows, width), BF16),
        pltpu.VMEM((done, 2, rows, width), BF16),
        pltpu.SemaphoreType.DMA((done, 6)),
        pltpu.SemaphoreType.DMA((done, 6)),
    ]
    if inner:
        out_specs += [
            pl.BlockSpec((tile, d), lambda c, t: (at_last(c, t), 0)),
            pl.BlockSpec((d, tile), lambda c, t: (0, at_last(c, t))),
        ]
        out_shape += [jax.ShapeDtypeStruct((tokens, d), BF16), jax.ShapeDtypeStruct((d, tokens), BF16)]
        scratch.append(pltpu.VMEM((d, tokens), F32))
    outs = pl.pallas_call(
        functools.partial(backward_kernel, n, chunks, tiles, carry, inner),
        grid=(chunks, tiles),
        in_specs=in_specs,
        out_specs=out_specs,
        out_shape=out_shape,
        scratch_shapes=scratch,
        compiler_params=pltpu.CompilerParams(
            vmem_limit_bytes=VMEM_LIMIT, collective_id=collective_id, has_side_effects=True,
            dimension_semantics=("arbitrary", "arbitrary"),
        ),
        name=f"backward{layer}",
    )(*args)
    sums = [tuple(outs[3 * i : 3 * i + 3]) for i in range(done)]
    return sums, outs[3 * done], outs[3 * done + 1 :]


def update_kernel(n, chunks, layers, count, *refs):
    refs = list(refs)
    take = lambda k: [refs.pop(0) for _ in range(k)]
    last_ref = take(1)[0]
    total_chunks = layers * chunks
    sums = [take(3) for _ in range(total_chunks - 1)]
    w_in, m_in, v_in = take(3), take(3), take(3)
    w_out, m_out, v_out = take(3), take(3), take(3)
    last_out = take(3)
    recv, summed, send_sem, recv_sem = take(4)
    w_own, m_own, v_own, w_new = take(3), take(3), take(3), take(3)
    ss_mine, ss_all, ss_send, ss_recv = take(4)
    load_sem, store_sem, gather_send, gather_recv = take(4)

    ring = Ring(n, recv, summed, send_sem, recv_sem)
    me = ring.me
    own_rows = [m.shape[1] for m in m_own]

    def mine(k, owner, h=None):
        rows = own_rows[k]
        if h is None:
            return pl.ds(pl.multiple_of(owner * rows, 16), rows)
        return pl.ds(pl.multiple_of(owner * rows + h * (rows // 2), 16), rows // 2)

    loads = []
    for k in range(3):
        for l in range(layers):
            i = len(loads)
            loads.append(
                (
                    pltpu.make_async_copy(w_in[k].at[l, mine(k, me)], w_own[k].at[l], load_sem.at[0, k, l]),
                    pltpu.make_async_copy(m_in[k].at[l], m_own[k].at[l], load_sem.at[1, k, l]),
                    pltpu.make_async_copy(v_in[k].at[l], v_own[k].at[l], load_sem.at[2, k, l]),
                )
            )
    for load in loads:
        for copy in load:
            copy.start()

    peers = [(me + i) % n for i in range(1, n)]
    greet(peers)
    ring.start(0, last_ref)
    ring.pass_on(0, last_ref)
    unpack(ring.finish(0, last_ref), n, *last_out)
    sums = sums[: (layers - 1) * chunks] + sums[(layers - 1) * chunks :] + [last_out]

    total = sums[0][2][...]
    for _, _, ss in sums[1:]:
        total = total + ss[...]
    ss_mine[...] = total
    shares = [
        pltpu.make_async_remote_copy(
            src_ref=ss_mine, dst_ref=ss_all.at[i], send_sem=ss_send.at[i], recv_sem=ss_recv.at[i],
            device_id={AXIS: peer}, device_id_type=MESH,
        )
        for i, peer in enumerate(peers)
    ]
    for share in shares:
        share.start()
    for share in shares:
        share.wait()
    for i in range(n - 1):
        total = total + ss_all[i]
    mean = jnp.sum(jnp.sum(total, axis=0, keepdims=True), axis=1, keepdims=True) / count
    factor = jnp.minimum(1.0, 0.5 * lax.rsqrt(mean + 1e-30))

    def gather(k, l, owner, h, way, src, to):
        return pltpu.make_async_remote_copy(
            src_ref=src,
            dst_ref=w_out[k].at[l, mine(k, owner, h)],
            send_sem=gather_send.at[k, l, h, way],
            recv_sem=gather_recv.at[k, l, h, way],
            device_id={AXIS: to},
            device_id_type=MESH,
        )

    def own_send(k, l, h, way):
        half = own_rows[k] // 2
        return gather(k, l, me, h, way, w_new[k].at[l, pl.ds(h * half, half)], (ring.right, ring.left)[way])

    def onward(k, l, way):
        owner, to = ((ring.left, ring.right), (ring.right, ring.left))[way]
        return gather(k, l, owner, way, 2, w_out[k].at[l, mine(k, owner, way)], to)

    stores = []
    order = [(k, l) for l in reversed(range(layers)) for k in range(3)]
    for k, l in order:
        for copy in loads[k * layers + l]:
            copy.wait()
        base = (layers - 1 - l) * chunks

        def step(rows, columns, g):
            g = g.astype(F32) * factor
            w, m, v = w_own[k][l, rows, columns].astype(F32), m_own[k][l, rows, columns], v_own[k][l, rows, columns]
            m = 0.9 * m + 0.1 * g
            v = 0.95 * v + 0.05 * g * g
            w_new[k][l, rows, columns] = (w - 0.02 * (m * lax.rsqrt(v + 1e-8) + 0.1 * w)).astype(BF16)
            m_own[k][l, rows, columns] = m
            v_own[k][l, rows, columns] = v

        for c in range(chunks):
            gu, gd, _ = sums[base + c]
            if k == 2:
                step(slice(c * LANES, (c + 1) * LANES), slice(None), gd[...])
            else:
                for o in range(n):
                    at = o * chunks * LANES + c * LANES
                    step(slice(None), slice(at, at + LANES), gu[k, :, o * LANES : (o + 1) * LANES])
        for h in range(2):
            for way in range(2):
                own_send(k, l, (h + way) % 2, way).start()
        for j, (src, dst) in enumerate(
            (
                (w_new[k].at[l], w_out[k].at[l, mine(k, me)]),
                (m_own[k].at[l], m_out[k].at[l]),
                (v_own[k].at[l], v_out[k].at[l]),
            )
        ):
            stores.append(pltpu.make_async_copy(src, dst, store_sem.at[j, k, l]))
            stores[-1].start()
    for k, l in order:
        for way in range(2):
            own_send(k, l, way, way).wait_recv()
            onward(k, l, way).start()
    for k, l in order:
        for way in range(2):
            own_send(k, l, 1 - way, way).wait_recv()
            onward(k, l, way).wait_recv()
            onward(k, l, way).wait_send()
            for h in range(2):
                own_send(k, l, h, way).wait_send()
    for store in stores:
        store.wait()


def update(n, last, sums, w, m, v, collective_id):
    layers = w[0].shape[0]
    chunks = w[0].shape[2] // n // LANES
    count = sum(t.size for t in w)
    packed = last.shape
    rows, width = packed[2:]
    vmem = pl.BlockSpec(memory_space=pltpu.VMEM)
    anywhere = pl.BlockSpec(memory_space=pl.ANY)
    flat = [t for one in sums for t in one]
    own = [t.shape for t in m]
    return pl.pallas_call(
        functools.partial(update_kernel, n, chunks, layers, count),
        in_specs=[vmem] * (1 + len(flat)) + [anywhere] * 9,
        out_specs=[anywhere] * 9,
        out_shape=[jax.ShapeDtypeStruct(t.shape, t.dtype) for t in (*w, *m, *v)],
        scratch_shapes=[
            pltpu.VMEM((2, w[0].shape[1] // n, width), BF16),
            pltpu.VMEM((LANES, w[0].shape[1]), BF16),
            pltpu.VMEM((8, LANES), F32),
            pltpu.VMEM((1, 6, rows, width), BF16),
            pltpu.VMEM((1, 2, rows, width), BF16),
            pltpu.SemaphoreType.DMA((1, 6)),
            pltpu.SemaphoreType.DMA((1, 6)),
            *[pltpu.VMEM(s, BF16) for s in own],
            *[pltpu.VMEM(s, F32) for s in own],
            *[pltpu.VMEM(s, F32) for s in own],
            *[pltpu.VMEM(s, BF16) for s in own],
            pltpu.VMEM((8, LANES), F32),
            pltpu.VMEM((n - 1, 8, LANES), F32),
            pltpu.SemaphoreType.DMA((n - 1,)),
            pltpu.SemaphoreType.DMA((n - 1,)),
            pltpu.SemaphoreType.DMA((3, 3, layers)),
            pltpu.SemaphoreType.DMA((3, 3, layers)),
            pltpu.SemaphoreType.DMA((3, layers, 2, 3)),
            pltpu.SemaphoreType.DMA((3, layers, 2, 3)),
        ],
        compiler_params=pltpu.CompilerParams(vmem_limit_bytes=VMEM_LIMIT, collective_id=collective_id, has_side_effects=True),
        name="update",
    )(last, *flat, *w, *m, *v)


def solution(mesh):
    n = mesh.shape[AXIS]

    def step(x, dy, *arrays):
        w, m, v = arrays[:3], arrays[3:6], arrays[6:9]
        x, dy = x.reshape(x.shape[-2:]), dy.reshape(dy.shape[-2:])
        a1, a1t, a2, a2t, h1t, dyt = forward(x, dy, *w, 0)
        sums2, last2, (dh, dht) = backward(n, a2, a2t, dy, dyt, *w, 1, h1t=h1t, collective_id=0)
        sums1, last1, _ = backward(n, a1, a1t, dh, dht, *w, 0, carried=last2, collective_id=1)
        sums = [*sums2, sums1[0], *sums1[1:]]
        return tuple(update(n, last1, sums, w, m, v, 2))

    whole, rows = P(None, None, None), P(None, AXIS, None)
    own, own_rows = P("rep", None, None), P("rep", AXIS, None)
    one = P(("rep", AXIS), None, None)
    return jax.shard_map(
        step,
        mesh=mesh,
        in_specs=(one, one, *[whole] * 3, *[rows] * 6),
        out_specs=(*[own] * 3, *[own_rows] * 6),
        check_vma=False,
    )
```

time: 644 us -> 370 us (0.57); the launches traced: 634 us -> 370 us
  Pallas kernels: 0 us -> 345 us
  matrix products: 262 us -> 0 us
  waiting for transfers between devices: 224 us -> 0 us
  other arithmetic: 88.2 us -> 0 us
  between operations: 17.8 us -> 0.69 us
  blocking collectives: 9.69 us -> 0 us
  local copies, waits for them, and re-layouts: 31.6 us -> 23.5 us
    pallas_call x0 -> x4, Pallas kernels: none -> 345 us  [the longest x2 182 us: backward(): pl.pallas_call(functools.partial(backward_kernel, n, chunks, tiles, carry...]
    dot_general x15 -> x0, matrix products: 262 us -> none  [the longest x5 95.7 us: layer(): gate = jnp.dot(a, w['w_gate'], preferred_element_type=jnp.float32)]
    reshape x3 -> x0, waiting for transfers between devices: 118 us -> none  [step(): t.reshape(-1, *t.shape[2:])]
    unnamed x15 -> x0, waiting for transfers between devices: 106 us -> none
    unnamed x4 -> x0, other arithmetic: 56.5 us -> none
    reshape x3 -> x0, other arithmetic: 17.3 us -> none  [step(): t.reshape(-1, *t.shape[2:])]
    reduce_sum x1 -> x0, blocking collectives: 9.69 us -> none  [of_a_group(): jnp.sum(g * g)]
    unnamed x37 -> x25, local copies, waits for them, and re-layouts: 31 us -> 23.5 us
  transfers between devices with their start and end apart: 9 -> 0, of which waited for: 6 -> 0; matrix products, arithmetic and copies ran while one was open for 36% -> 0% of each run, Pallas kernels for 0% -> 0%
where the time goes in v1:
time: 370 us
  Pallas kernels  345 us (93%)
  local copies, waits for them, and re-layouts  23.5 us (6%)
    pallas_call x2, Pallas kernels, backward(): pl.pallas_call(functools.partial(backward_kernel, n, chunks, tiles, carry...  182 us
    pallas_call x1, Pallas kernels, update(): pl.pallas_call(functools.partial(update_kernel, n, chunks, layers, count)...  123 us
    pallas_call x1, Pallas kernels, forward(): pl.pallas_call(forward_kernel, grid=(tokens // tile,), in_specs=[rows, ro...  40.8 us
    unnamed x25, local copies, waits for them, and re-layouts  23.5 us

profile of v1, /device:TPU:112, one launch (start us, length us, event | category | flops | bytes accessed | tf_op | source)
XLA Modules:
  0.0 369.5 jit_solution(16876969445030646378)
XLA Ops:
  0.6 40.8 %forward.1 = (bf16[4096,640]{1,0:T(8,128)(2,1)}, bf16[640,4096]{1,0:T(8,128)(2,1)}, bf16[4096,640]{1,0:T(8,128)(2,1)}, bf16[640,4096]{1,0:T(8,128)(2,1)}, bf16[6...) custom-call(bf16[4096,640]{1,0:T(8,128)(2,1)} %bitcast.4, bf16[4096,640]{1,0:T(8,128)(2,1)} %bitcast.2, ...), custom_call_target="tpu_custom_call" | custom-call | tf_op jit(solution)/shard_map/forward/pallas_call | solution.py:64
  41.5 105.3 %backward1.1 = (bf16[2,160,512]{2,1,0:T(8,128)(2,1)}, bf16[128,640]{1,0:T(8,128)(2,1)}, f32[8,128]{1,0:T(8,128)}, bf16[2,160,512]{2,1,0:T(8,128)(2,1)}, bf16[128...) custom-call(bf16[4096,640]{1,0:T(8,128)(2,1)} %get-tuple-element.36., ...), custom_call_target="tpu_custom_call" | custom-call | tf_op jit(solution)/shard_map/backward1/pallas_call | solution.py:304
  146.8 76.7 %backward0.1 = (bf16[2,160,512]{2,1,0:T(8,128)(2,1)}, bf16[128,640]{1,0:T(8,128)(2,1)}, f32[8,128]{1,0:T(8,128)}, bf16[2,160,512]{2,1,0:T(8,128)(2,1)}, bf16[128...) custom-call(bf16[4096,640]{1,0:T(8,128)(2,1)} %get-tuple-element.34., ...), custom_call_target="tpu_custom_call" | custom-call | tf_op jit(solution)/shard_map/backward0/pallas_call | solution.py:304
  223.5 122.6 %update.1 = (bf16[2,640,1536]{2,1,0:T(8,128)(2,1)}, bf16[2,640,1536]{2,1,0:T(8,128)(2,1)}, bf16[2,1536,640]{2,1,0:T(8,128)(2,1)}, f32[2,160,1536]{2,1,0:T(8,128)...) custom-call(bf16[4,2,240,512]{3,2,1,0:T(8,128)(2,1)} %get-tuple-elem, ...), custom_call_target="tpu_custom_call" | custom-call | tf_op jit(solution)/shard_map/update/pallas_call | solution.py:466
  346.0 0.0 copy-start.1
  346.0 4.5 %copy.29 = bf16[2,640,1536]{2,1,0:T(8,128)(2,1)} copy(bf16[2,640,1536]{2,1,0:T(8,128)(2,1)} %get-tuple-element.68) | data formatting | bytes 7864320
  350.5 0.0 copy-done.1
  350.5 0.0 copy-start
  350.5 2.0 copy.30
  352.5 1.5 copy-done
  354.0 0.0 copy-start.7
  354.0 2.0 copy.31
  356.0 1.0 copy-done.7
  357.0 0.0 copy-start.6
  357.0 1.3 copy.32
  358.3 1.0 copy-done.6
  359.2 0.0 copy-start.5
  359.2 1.3 copy.33
  360.5 1.0 copy-done.5
  361.5 0.0 copy-start.4
  361.5 1.3 copy.34
  362.8 1.0 copy-done.4
  363.8 0.0 copy-start.3
  363.8 1.3 copy.35
  365.0 1.0 copy-done.3
  366.0 0.0 copy-start.2
  366.0 1.3 copy.36
  367.3 1.0 copy-done.2
  368.3 1.3 copy.37
Async XLA Ops:
  346.0 4.5 %copy-start.1 = (bf16[2,640,1536]{2,1,0:T(8,128)(2,1)S(1)}, bf16[2,640,1536]{2,1,0:T(8,128)(2,1)}, u32[]{:S(2)}) copy-start(bf16[2,640,1536]{2,1,0:T(8,128)(2,1)} %get-tuple-element.69) | copy-start | bytes 11796484
  350.5 3.5 copy-start
  354.0 3.0 copy-start.7
  357.0 2.3 copy-start.6
  359.2 2.3 copy-start.5
  361.5 2.3 copy-start.4
  363.8 2.3 copy-start.3
  366.0 2.3 copy-start.2

commit v2 on v1

--- a/solution.py
+++ b/solution.py
@@ -12,6 +12,10 @@
 AXIS = "dp"
 MESH = pl.DeviceIdType.MESH
 VMEM_LIMIT = 64000 * 1024
+VMEM, RESERVE = 64 * 1024 * 1024, 192 * 1024
+SUB = 256
+SUB_BACK = 512
+TILE_INNER = 2048
 ROWS, COLS = (((0,), (0,)), ((), ())), (((1,), (1,)), ((), ()))
 
 
@@ -32,44 +36,103 @@
     return (wide * scale).astype(BF16)
 
 
-def forward_kernel(x_ref, dy_ref, wg_ref, wu_ref, wd_ref, a1_ref, a1t_ref, a2_ref, a2t_ref, h1t_ref, dyt_ref):
-    ff = wg_ref.shape[1]
-    part = 512
-    dyt_ref[...] = dy_ref[...].T
-    x = x_ref[...].astype(F32)
-    a1 = normed(x, -1)
-    a1_ref[...] = a1
-    a1t_ref[...] = a1.T
-    down = None
-    for f in range(0, ff, part):
-        gate = dot(a1, wg_ref[:, f : f + part])
-        up = dot(a1, wu_ref[:, f : f + part])
+def fetch(w_refs, layer, n, chunk, buffers, sems):
+    copies = []
+    for k, (w, buffer) in enumerate(zip(w_refs, buffers)):
+        if buffer is None:
+            continue
+        own = w.shape[1 if k == 2 else 2] // n
+        for o in range(n):
+            there = pl.ds(pl.multiple_of(o * own + chunk * LANES, LANES), LANES)
+            here = pl.ds(o * LANES, LANES)
+            if k == 2:
+                copies.append(pltpu.make_async_copy(w.at[layer, there, :], buffer.at[here, :], sems.at[k, o]))
+            else:
+                copies.append(pltpu.make_async_copy(w.at[layer, :, there], buffer.at[:, here], sems.at[k, o]))
+    return copies
+
+
+def forward_kernel(n, layer, x_ref, dy_ref, wg_ref, wu_ref, wd_ref, a1t_ref, a2_ref, a2t_ref, h1t_ref, dyt_ref, gate_ref, up_ref, wg, wu, wd, w_sem):
+    chunks = wg.shape[0]
+    parts = x_ref.shape[0] // SUB
+
+    def weights(c):
+        return fetch((wg_ref, wu_ref, wd_ref), layer, n, c, (wg.at[c], wu.at[c], wd.at[c]), w_sem.at[c])
+
+    @pl.when(pl.program_id(0) == 0)
+    def _():
+        for c in range(chunks):
+            for copy in weights(c):
+                copy.start()
+        for c in range(chunks):
+            for copy in weights(c):
+                copy.wait()
+
+    def before(p):
+        here = slice(p * SUB, (p + 1) * SUB)
+        a1 = normed(x_ref[here, :].astype(F32), -1)
+        a1t_ref[:, here] = a1.T
+        dyt_ref[:, here] = dy_ref[here, :].T
+        return a1
+
+    def first(p, a1, c):
+        here = slice(p * SUB, (p + 1) * SUB)
+        gate, up = dot(a1, wg[c]), dot(a1, wu[c])
+        gate_ref[c, here, :] = gate
+        up_ref[c, here, :] = up
+        return gate, up
+
+    def after(p, down):
+        here = slice(p * SUB, (p + 1) * SUB)
+        h1 = (x_ref[here, :].astype(F32) + down.astype(BF16).astype(F32)).astype(BF16)
+        h1t_ref[:, here] = h1.T
+        a2 = normed(h1.astype(F32), -1)
+        a2_ref[here, :] = a2
+        a2t_ref[:, here] = a2.T
+
+    todo = [(p, c) for p in range(parts) for c in range(chunks)]
+    a1 = before(0)
+    ahead, down = first(0, a1, 0), None
+    for i, (p, c) in enumerate(todo):
+        gate, up = ahead
+        if i + 1 < len(todo):
+            q, e = todo[i + 1]
+            if q != p:
+                a1 = before(q)
+            ahead = first(q, a1, e)
         hidden = (gate * sigmoid(gate) * up).astype(BF16)
-        term = dot(hidden, wd_ref[f : f + part, :])
-        down = term if down is None else down + term
-    h1 = (x + down.astype(BF16).astype(F32)).astype(BF16)
-    h1t_ref[...] = h1.T
-    a2 = normed(h1.astype(F32), -1)
-    a2_ref[...] = a2
-    a2t_ref[...] = a2.T
-
-
-def forward(x, dy, wg, wu, wd, layer, tile=512):
+        term = dot(hidden, wd[c])
+        down = term if c == 0 else down + term
+        if c + 1 == chunks:
+            after(p, down)
+
+
+def forward(n, x, dy, w, layer, tile=512):
     tokens, d = x.shape
-    ff = wg.shape[-1]
+    ff = w[0].shape[-1]
+    width = n * LANES
+    chunks = ff // width
     rows = pl.BlockSpec((tile, d), lambda t: (t, 0))
     columns = pl.BlockSpec((d, tile), lambda t: (0, t))
-    weight = lambda a, b: pl.BlockSpec((None, a, b), lambda t: (layer, 0, 0))
+    inside = pl.BlockSpec((chunks, tile, width), lambda t: (0, t, 0))
+    weight = pl.BlockSpec(memory_space=pltpu.HBM)
     straight, turned = jax.ShapeDtypeStruct((tokens, d), BF16), jax.ShapeDtypeStruct((d, tokens), BF16)
+    kept = jax.ShapeDtypeStruct((chunks, tokens, width), F32)
     return pl.pallas_call(
-        forward_kernel,
+        functools.partial(forward_kernel, n, layer),
         grid=(tokens // tile,),
-        in_specs=[rows, rows, weight(d, ff), weight(d, ff), weight(ff, d)],
-        out_specs=[rows, columns, rows, columns, columns, columns],
-        out_shape=[straight, turned, straight, turned, turned, turned],
+        in_specs=[rows, rows, weight, weight, weight],
+        out_specs=[columns, rows, columns, columns, columns, inside, inside],
+        out_shape=[turned, straight, turned, turned, turned, kept, kept],
+        scratch_shapes=[
+            pltpu.VMEM((chunks, d, width), BF16),
+            pltpu.VMEM((chunks, d, width), BF16),
+            pltpu.VMEM((chunks, width, d), BF16),
+            pltpu.SemaphoreType.DMA((chunks, 3, n)),
+        ],
         compiler_params=pltpu.CompilerParams(vmem_limit_bytes=VMEM_LIMIT),
         name="forward",
-    )(x, dy, wg, wu, wd)
+    )(x, dy, *w)
 
 
 class Ring:
@@ -162,22 +225,31 @@
     pl.semaphore_wait(barrier, len(peers))
 
 
-def backward_kernel(n, chunks, tiles, carried, inner, *refs):
+def backward_kernel(n, chunks, tiles, carried, inner, layer, *refs):
     refs = list(refs)
     take = lambda count: [refs.pop(0) for _ in range(count)]
-    a_ref, at_ref, dy_ref, dyt_ref, wg_ref, wu_ref, wd_ref = take(7)
-    h1t_ref = take(1)[0] if inner else None
+    at_ref = take(1)[0]
+    if inner:
+        a_ref, dy_ref, dyt_ref = take(3)
+        tile = a_ref.shape[0]
+    else:
+        gate_ref, up_ref, dat_in, h1t_ref, outer_ref = take(5)
+        tile = gate_ref.shape[0]
+    w_refs = take(3)
     carried_ref = take(1)[0] if carried else None
     done = chunks - 1 + carried
     outs = [take(3) for _ in range(done)]
     last_ref = take(1)[0]
-    dh_ref, dht_ref = take(2) if inner else (None, None)
+    dat_out = take(1)[0] if inner else None
     acc_g, acc_u, acc_d, blocks, recv, summed, send_sem, recv_sem = take(8)
-    dat_ref = take(1)[0] if inner else None
+    wd_now, w_sem = take(2)
+    wg_now, wu_now = take(2) if inner else (None, None)
+    if inner:
+        dat_ref, dat_sem = take(2)
+    else:
+        dh_ref, dht_ref = take(2)
 
     c, t = pl.program_id(0), pl.program_id(1)
-    tile = a_ref.shape[0]
-    own = wg_ref.shape[1] // n
     ring = Ring(n, recv, summed, send_sem, recv_sem)
 
     @pl.when((c == 0) & (t == 0))
@@ -186,20 +258,31 @@
         if carried:
             ring.start(0, carried_ref)
 
-    places = [pl.ds(pl.multiple_of(o * own + c * LANES, LANES), LANES) for o in range(n)]
-    wg = jnp.concatenate([wg_ref[:, p] for p in places], axis=1)
-    wu = jnp.concatenate([wu_ref[:, p] for p in places], axis=1)
-    wd = jnp.concatenate([wd_ref[p, :] for p in places], axis=0)
-
-    a, dy = a_ref[...], dy_ref[...]
-    gate, up = dot(a, wg), dot(a, wu)
-    dhidden = dot_t(dy, wd).astype(BF16).astype(F32)
-    s = sigmoid(gate)
-    silu = gate * s
-    hidden = (silu * up).astype(BF16)
-    dup = (dhidden * silu).astype(BF16)
-    dgate = (dhidden * up * (s + silu * (1 - s))).astype(BF16)
-    at, dyt = at_ref[...], dyt_ref[...]
+    def weights(chunk, slot):
+        buffers = [None if now is None else now.at[slot] for now in (wg_now, wu_now, wd_now)]
+        return fetch(w_refs, layer, n, chunk, buffers, w_sem.at[slot])
+
+    slot = c % 2
+
+    @pl.when((c == 0) & (t == 0))
+    def _():
+        for copy in weights(0, 0):
+            copy.start()
+
+    @pl.when(t == 0)
+    def _():
+        for copy in weights(c, slot):
+            copy.wait()
+
+    @pl.when((t == 0) & (c < chunks - 1))
+    def _():
+        for copy in weights(c + 1, 1 - slot):
+            copy.start()
+
+    wd = wd_now.at[slot]
+    if inner:
+        wg, wu = wg_now.at[slot], wu_now.at[slot]
+
     accs = acc_g, acc_u, acc_d
 
     @pl.when(t == 0)
@@ -207,41 +290,91 @@
         for acc in accs:
             acc[...] = jnp.zeros_like(acc)
 
-    acc_g[...] += dot(at, dgate)
-    acc_u[...] += dot(at, dup)
-    acc_d[...] += dot(dyt, hidden)
-
     if inner:
-        here = pl.ds(pl.multiple_of(t * tile, tile), tile)
 
         @pl.when(c == 0)
         def _():
-            dat_ref[:, here] = jnp.zeros((dat_ref.shape[0], tile), F32)
-
-        dat_ref[:, here] += dot_t(wg, dgate) + dot_t(wu, dup)
+            dat_ref[:, pl.ds(pl.multiple_of(t * tile, tile), tile)] = jnp.zeros((dat_ref.shape[0], tile), F32)
+
+    else:
+
+        @pl.when(c == 0)
+        def _():
+            for p in range(tile // LANES // 2):
+                here = slice(p * 2 * LANES, (p + 1) * 2 * LANES)
+                there = pl.ds(pl.multiple_of(t * tile + p * 2 * LANES, 2 * LANES), 2 * LANES)
+                da = dat_in[:, here].astype(BF16).astype(F32)
+                wide = h1t_ref[:, here].astype(F32)
+                scale = lax.rsqrt(jnp.mean(wide * wide, 0, keepdims=True) + 1e-6)
+                along = jnp.mean(da * wide, 0, keepdims=True)
+                dwide = da * scale - wide * (scale * scale * scale * along)
+                dht = (outer_ref[:, here].astype(F32) + dwide.astype(BF16).astype(F32)).astype(BF16)
+                dht_ref[:, there] = dht
+                dh_ref[there, :] = dht.T
+
+    sub = min(tile, SUB_BACK)
+
+    def first(p):
+        rows = slice(p * sub, (p + 1) * sub)
+        if not inner:
+            there = pl.ds(pl.multiple_of(t * tile + p * sub, sub), sub)
+            return gate_ref[rows, :], up_ref[rows, :], dot_t(dh_ref[there, :], wd[...])
+        dhidden = dot_t(dy_ref[rows, :], wd[...])
+        a = a_ref[rows, :]
+        return dot(a, wg[...]), dot(a, wu[...]), dhidden
+
+    def middle(gate, up, dhidden):
+        dhidden = dhidden.astype(BF16).astype(F32)
+        s = sigmoid(gate)
+        silu = gate * s
+        return (silu * up).astype(BF16), (dhidden * silu).astype(BF16), (dhidden * up * (s + silu * (1 - s))).astype(BF16)
+
+    def second(p, hidden, dup, dgate):
+        columns = slice(p * sub, (p + 1) * sub)
+        here = pl.ds(pl.multiple_of(t * tile + p * sub, sub), sub)
+        if inner:
+            dat_ref[:, here] += dot_t(wg[...], dgate) + dot_t(wu[...], dup)
+        at = at_ref[:, columns]
+        acc_g[...] += dot(at, dgate)
+        acc_u[...] += dot(at, dup)
+        dyt = dyt_ref[:, columns] if inner else dht_ref[:, here]
+        acc_d[...] += dot(dyt, hidden)
+
+    parts = tile // sub
+    ahead = first(0)
+    for p in range(parts):
+        now = ahead
+        if p + 1 < parts:
+            ahead = first(p + 1)
+        second(p, *middle(*now))
+
+    if inner:
+
+        def keep(tile_number):
+            here = pl.ds(pl.multiple_of(tile_number * tile, tile), tile)
+            return pltpu.make_async_copy(dat_ref.at[:, here], dat_out.at[:, here], dat_sem.at[tile_number])
 
         @pl.when(c == chunks - 1)
         def _():
-            da = dat_ref[:, here].astype(BF16).astype(F32)
-            wide = h1t_ref[...].astype(F32)
-            scale = lax.rsqrt(jnp.mean(wide * wide, 0, keepdims=True) + 1e-6)
-            along = jnp.mean(da * wide, 0, keepdims=True)
-            dwide = da * scale - wide * (scale * scale * scale * along)
-            dht = (dyt.astype(F32) + dwide.astype(BF16).astype(F32)).astype(BF16)
-            dht_ref[...] = dht
-            dh_ref[...] = dht.T
+            keep(t).start()
+
+        @pl.when((c == chunks - 1) & (t == tiles - 1))
+        def _():
+            for tile_number in range(tiles):
+                keep(tile_number).wait()
 
     for step in range(chunks):
         i = step - 1 + carried
         if i < 0:
             continue
         source = carried_ref if carried and i == 0 else blocks.at[i - carried]
+        over = (c == step) & (t == tiles - 1) if step == chunks - 1 else (c == step + 1) & (t == 0)
 
         @pl.when((c == step) & (t == tiles // 2 - 1))
         def _():
             ring.pass_on(i, source)
 
-        @pl.when((c == step) & (t == tiles - 1))
+        @pl.when(over)
         def _():
             unpack(ring.finish(i, source), n, *outs[i])
 
@@ -257,26 +390,28 @@
         pack(last_ref, n, *accs)
 
 
-def backward(n, a, at, dy, dyt, wg, wu, wd, layer, h1t=None, carried=None, tile=1024, collective_id=0):
-    tokens, d = a.shape
-    ff = wg.shape[-1]
-    chunks = ff // n // LANES
+def backward(n, at, w, layer, outer=None, kept=None, carried=None, tile=1024, collective_id=0):
+    d, tokens = at.shape
+    ff = w[0].shape[-1]
+    width, rows = n * LANES, 3 * (d // n // 2)
+    chunks = ff // width
     tiles = tokens // tile
-    inner, carry = h1t is not None, int(carried is not None)
-    width, rows = n * LANES, 3 * (d // n // 2)
+    inner, carry = kept is None, int(carried is not None)
     done = chunks - 1 + carry
     straight = pl.BlockSpec((tile, d), lambda c, t: (t, 0))
     turned = pl.BlockSpec((d, tile), lambda c, t: (0, t))
-    weight = lambda a, b: pl.BlockSpec((None, a, b), lambda c, t: (layer, 0, 0), pipeline_mode=pl.Buffered(1))
+    at_first = pl.BlockSpec((d, tile), lambda c, t: (0, jnp.where(c == 0, t, tiles - 1)))
+    inside = pl.BlockSpec((None, tile, width), lambda c, t: (c, t, 0))
+    hbm = pl.BlockSpec(memory_space=pltpu.HBM)
     whole = lambda *shape: pl.BlockSpec(shape, lambda c, t: (0,) * len(shape))
     once = lambda *shape: pl.BlockSpec(shape, lambda c, t: (0,) * len(shape), pipeline_mode=pl.Buffered(1))
-    at_last = lambda c, t: jnp.where(c == chunks - 1, t, 0)
     packed = (n, 2, rows, width)
-    in_specs = [straight, turned, straight, turned, weight(d, ff), weight(d, ff), weight(ff, d)]
-    args = [a, at, dy, dyt, wg, wu, wd]
     if inner:
-        in_specs.append(pl.BlockSpec((d, tile), lambda c, t: (0, at_last(c, t))))
-        args.append(h1t)
+        in_specs = [turned, straight, straight, turned, hbm, hbm, hbm]
+        args = [at, *outer, *w]
+    else:
+        in_specs = [turned, inside, inside, at_first, at_first, at_first, hbm, hbm, hbm]
+        args = [at, *kept, *w]
     if carry:
         in_specs.append(once(*packed))
         args.append(carried)
@@ -293,16 +428,22 @@
         pltpu.VMEM((done, 2, rows, width), BF16),
         pltpu.SemaphoreType.DMA((done, 6)),
         pltpu.SemaphoreType.DMA((done, 6)),
+        pltpu.VMEM((2, width, d), BF16),
+        pltpu.SemaphoreType.DMA((2, 3, n)),
     ]
     if inner:
-        out_specs += [
-            pl.BlockSpec((tile, d), lambda c, t: (at_last(c, t), 0)),
-            pl.BlockSpec((d, tile), lambda c, t: (0, at_last(c, t))),
+        out_specs.append(hbm)
+        out_shape.append(jax.ShapeDtypeStruct((d, tokens), F32))
+        scratch += [
+            pltpu.VMEM((2, d, width), BF16),
+            pltpu.VMEM((2, d, width), BF16),
+            pltpu.VMEM((d, tokens), F32),
+            pltpu.SemaphoreType.DMA((tiles,)),
         ]
-        out_shape += [jax.ShapeDtypeStruct((tokens, d), BF16), jax.ShapeDtypeStruct((d, tokens), BF16)]
-        scratch.append(pltpu.VMEM((d, tokens), F32))
+    else:
+        scratch += [pltpu.VMEM((tokens, d), BF16), pltpu.VMEM((d, tokens), BF16)]
     outs = pl.pallas_call(
-        functools.partial(backward_kernel, n, chunks, tiles, carry, inner),
+        functools.partial(backward_kernel, n, chunks, tiles, carry, inner, layer),
         grid=(chunks, tiles),
         in_specs=in_specs,
         out_specs=out_specs,
@@ -322,15 +463,15 @@
     refs = list(refs)
     take = lambda k: [refs.pop(0) for _ in range(k)]
     last_ref = take(1)[0]
-    total_chunks = layers * chunks
-    sums = [take(3) for _ in range(total_chunks - 1)]
+    before = layers * chunks - 1
+    sums_in = [take(3) for _ in range(before)]
     w_in, m_in, v_in = take(3), take(3), take(3)
-    w_out, m_out, v_out = take(3), take(3), take(3)
-    last_out = take(3)
+    w_out, m_own, v_own = take(3), take(3), take(3)
+    last, gu_all, gd_all, squares = take(4)
     recv, summed, send_sem, recv_sem = take(4)
-    w_own, m_own, v_own, w_new = take(3), take(3), take(3), take(3)
+    w_own = take(3)
     ss_mine, ss_all, ss_send, ss_recv = take(4)
-    load_sem, store_sem, gather_send, gather_recv = take(4)
+    load_sem, sums_sem, last_sem, gather_send, gather_recv = take(5)
 
     ring = Ring(n, recv, summed, send_sem, recv_sem)
     me = ring.me
@@ -357,16 +498,28 @@
         for copy in load:
             copy.start()
 
+    sum_loads = [
+        pltpu.make_async_copy(src, dst.at[i], sums_sem.at[i, j])
+        for i, one in enumerate(sums_in)
+        for j, (src, dst) in enumerate(zip(one, (gu_all, gd_all, squares)))
+    ]
+    last_load = pltpu.make_async_copy(last_ref, last, last_sem)
+    last_load.start()
+    for copy in sum_loads:
+        copy.start()
+
     peers = [(me + i) % n for i in range(1, n)]
     greet(peers)
-    ring.start(0, last_ref)
-    ring.pass_on(0, last_ref)
-    unpack(ring.finish(0, last_ref), n, *last_out)
-    sums = sums[: (layers - 1) * chunks] + sums[(layers - 1) * chunks :] + [last_out]
-
-    total = sums[0][2][...]
-    for _, _, ss in sums[1:]:
-        total = total + ss[...]
+    last_load.wait()
+    ring.start(0, last)
+    for copy in sum_loads:
+        copy.wait()
+    ring.pass_on(0, last)
+    unpack(ring.finish(0, last), n, gu_all.at[before], gd_all.at[before], squares.at[before])
+
+    total = squares[0]
+    for i in range(before):
+        total = total + squares[i + 1]
     ss_mine[...] = total
     shares = [
         pltpu.make_async_remote_copy(
@@ -395,14 +548,12 @@
         )
 
     def own_send(k, l, h, way):
-        half = own_rows[k] // 2
-        return gather(k, l, me, h, way, w_new[k].at[l, pl.ds(h * half, half)], (ring.right, ring.left)[way])
+        return gather(k, l, me, h, way, w_out[k].at[l, mine(k, me, h)], (ring.right, ring.left)[way])
 
     def onward(k, l, way):
         owner, to = ((ring.left, ring.right), (ring.right, ring.left))[way]
         return gather(k, l, owner, way, 2, w_out[k].at[l, mine(k, owner, way)], to)
 
-    stores = []
     order = [(k, l) for l in reversed(range(layers)) for k in range(3)]
     for k, l in order:
         for copy in loads[k * layers + l]:
@@ -414,30 +565,21 @@
             w, m, v = w_own[k][l, rows, columns].astype(F32), m_own[k][l, rows, columns], v_own[k][l, rows, columns]
             m = 0.9 * m + 0.1 * g
             v = 0.95 * v + 0.05 * g * g
-            w_new[k][l, rows, columns] = (w - 0.02 * (m * lax.rsqrt(v + 1e-8) + 0.1 * w)).astype(BF16)
+            there = pl.ds(pl.multiple_of(me * own_rows[k] + rows.start, 16), rows.stop - rows.start)
+            w_out[k][l, there, columns] = (w - 0.02 * (m * lax.rsqrt(v + 1e-8) + 0.1 * w)).astype(BF16)
             m_own[k][l, rows, columns] = m
             v_own[k][l, rows, columns] = v
 
         for c in range(chunks):
-            gu, gd, _ = sums[base + c]
             if k == 2:
-                step(slice(c * LANES, (c + 1) * LANES), slice(None), gd[...])
+                step(slice(c * LANES, (c + 1) * LANES), slice(None), gd_all[base + c])
             else:
                 for o in range(n):
                     at = o * chunks * LANES + c * LANES
-                    step(slice(None), slice(at, at + LANES), gu[k, :, o * LANES : (o + 1) * LANES])
+                    step(slice(0, own_rows[k]), slice(at, at + LANES), gu_all[base + c, k, :, o * LANES : (o + 1) * LANES])
         for h in range(2):
             for way in range(2):
                 own_send(k, l, (h + way) % 2, way).start()
-        for j, (src, dst) in enumerate(
-            (
-                (w_new[k].at[l], w_out[k].at[l, mine(k, me)]),
-                (m_own[k].at[l], m_out[k].at[l]),
-                (v_own[k].at[l], v_out[k].at[l]),
-            )
-        ):
-            stores.append(pltpu.make_async_copy(src, dst, store_sem.at[j, k, l]))
-            stores[-1].start()
     for k, l in order:
         for way in range(2):
             own_send(k, l, way, way).wait_recv()
@@ -449,8 +591,6 @@
             onward(k, l, way).wait_send()
             for h in range(2):
                 own_send(k, l, h, way).wait_send()
-    for store in stores:
-        store.wait()
 
 
 def update(n, last, sums, w, m, v, collective_id):
@@ -460,38 +600,59 @@
     packed = last.shape
     rows, width = packed[2:]
     vmem = pl.BlockSpec(memory_space=pltpu.VMEM)
-    anywhere = pl.BlockSpec(memory_space=pl.ANY)
+    hbm = pl.BlockSpec(memory_space=pltpu.HBM)
     flat = [t for one in sums for t in one]
     own = [t.shape for t in m]
+    many = layers * chunks
     return pl.pallas_call(
         functools.partial(update_kernel, n, chunks, layers, count),
-        in_specs=[vmem] * (1 + len(flat)) + [anywhere] * 9,
-        out_specs=[anywhere] * 9,
-        out_shape=[jax.ShapeDtypeStruct(t.shape, t.dtype) for t in (*w, *m, *v)],
+        in_specs=[hbm] * (1 + len(flat) + 9),
+        out_specs=[vmem] * 9,
+        out_shape=[pltpu.VMEM(t.shape, t.dtype) for t in (*w, *m, *v)],
         scratch_shapes=[
-            pltpu.VMEM((2, w[0].shape[1] // n, width), BF16),
-            pltpu.VMEM((LANES, w[0].shape[1]), BF16),
-            pltpu.VMEM((8, LANES), F32),
+            pltpu.VMEM(packed, BF16),
+            pltpu.VMEM((many, 2, w[0].shape[1] // n, width), BF16),
+            pltpu.VMEM((many, LANES, w[0].shape[1]), BF16),
+            pltpu.VMEM((many, 8, LANES), F32),
             pltpu.VMEM((1, 6, rows, width), BF16),
             pltpu.VMEM((1, 2, rows, width), BF16),
             pltpu.SemaphoreType.DMA((1, 6)),
             pltpu.SemaphoreType.DMA((1, 6)),
-            *[pltpu.VMEM(s, BF16) for s in own],
-            *[pltpu.VMEM(s, F32) for s in own],
-            *[pltpu.VMEM(s, F32) for s in own],
             *[pltpu.VMEM(s, BF16) for s in own],
             pltpu.VMEM((8, LANES), F32),
             pltpu.VMEM((n - 1, 8, LANES), F32),
             pltpu.SemaphoreType.DMA((n - 1,)),
             pltpu.SemaphoreType.DMA((n - 1,)),
             pltpu.SemaphoreType.DMA((3, 3, layers)),
-            pltpu.SemaphoreType.DMA((3, 3, layers)),
+            pltpu.SemaphoreType.DMA((many - 1, 3)),
+            pltpu.SemaphoreType.DMA,
             pltpu.SemaphoreType.DMA((3, layers, 2, 3)),
             pltpu.SemaphoreType.DMA((3, layers, 2, 3)),
         ],
-        compiler_params=pltpu.CompilerParams(vmem_limit_bytes=VMEM_LIMIT, collective_id=collective_id, has_side_effects=True),
+        compiler_params=pltpu.CompilerParams(vmem_limit_bytes=VMEM - RESERVE - sum(t.size * t.dtype.itemsize for t in (*w, *m, *v)), collective_id=collective_id, has_side_effects=True),
         name="update",
     )(last, *flat, *w, *m, *v)
+
+
+def put_kernel(count, *refs):
+    sources, targets, sem = refs[:count], refs[count : 2 * count], refs[2 * count]
+    copies = [pltpu.make_async_copy(a, b, sem.at[i]) for i, (a, b) in enumerate(zip(sources, targets))]
+    for copy in copies:
+        copy.start()
+    for copy in copies:
+        copy.wait()
+
+
+def put(arrays):
+    return pl.pallas_call(
+        functools.partial(put_kernel, len(arrays)),
+        in_specs=[pl.BlockSpec(memory_space=pltpu.VMEM)] * len(arrays),
+        out_specs=[pl.BlockSpec(memory_space=pltpu.HBM)] * len(arrays),
+        out_shape=[jax.ShapeDtypeStruct(t.shape, t.dtype) for t in arrays],
+        scratch_shapes=[pltpu.SemaphoreType.DMA((len(arrays),))],
+        compiler_params=pltpu.CompilerParams(vmem_limit_bytes=16 * 1024 * 1024),
+        name="put",
+    )(*arrays)
 
 
 def solution(mesh):
@@ -500,11 +661,11 @@
     def step(x, dy, *arrays):
         w, m, v = arrays[:3], arrays[3:6], arrays[6:9]
         x, dy = x.reshape(x.shape[-2:]), dy.reshape(dy.shape[-2:])
-        a1, a1t, a2, a2t, h1t, dyt = forward(x, dy, *w, 0)
-        sums2, last2, (dh, dht) = backward(n, a2, a2t, dy, dyt, *w, 1, h1t=h1t, collective_id=0)
-        sums1, last1, _ = backward(n, a1, a1t, dh, dht, *w, 0, carried=last2, collective_id=1)
-        sums = [*sums2, sums1[0], *sums1[1:]]
-        return tuple(update(n, last1, sums, w, m, v, 2))
+        a1t, a2, a2t, h1t, dyt, *kept = forward(n, x, dy, w, 0)
+        sums2, last2, (dat,) = backward(n, a2t, w, 1, outer=(a2, dy, dyt), tile=TILE_INNER, collective_id=0)
+        sums1, last1, _ = backward(n, a1t, w, 0, kept=(*kept, dat, h1t, dyt), carried=last2, collective_id=1)
+        sums = [*sums2, *sums1]
+        return tuple(put(update(n, last1, sums, w, m, v, 2)))
 
     whole, rows = P(None, None, None), P(None, AXIS, None)
     own, own_rows = P("rep", None, None), P("rep", AXIS, None)

time: 370 us -> 335 us (0.905)
  local copies, waits for them, and re-layouts: 23.5 us -> 0 us
  Pallas kernels: 345 us -> 334 us
    unnamed x25 -> x0, local copies, waits for them, and re-layouts: 23.5 us -> none
    pallas_call x2, Pallas kernels: 182 us -> 159 us  [backward(): pl.pallas_call(functools.partial(backward_kernel, n, chunks, tiles, carry...]
    pallas_call x1 -> x2, Pallas kernels: 40.8 us -> 50.8 us  [the longest x1 42.7 us: forward(): pl.pallas_call(functools.partial(forward_kernel, n, layer), grid=(tokens...]
where the time goes in v2:
time: 335 us
  Pallas kernels  334 us (100%)
    pallas_call x2, Pallas kernels, backward(): pl.pallas_call(functools.partial(backward_kernel, n, chunks, tiles, carry...  159 us
    pallas_call x1, Pallas kernels, update(): pl.pallas_call(functools.partial(update_kernel, n, chunks, layers, count)...  125 us
    pallas_call x1, Pallas kernels, forward(): pl.pallas_call(functools.partial(forward_kernel, n, layer), grid=(tokens...  42.7 us
    pallas_call x1, Pallas kernels, put(): pl.pallas_call(functools.partial(put_kernel, len(arrays)), in_specs=[pl.B...  8.09 us

profile of v2, /device:TPU:112, one launch (start us, length us, event | category | flops | bytes accessed | tf_op | source)
XLA Modules:
  0.0 335.1 jit_solution(13262751787557340092)
XLA Ops:
  0.6 42.7 %forward.1 = (bf16[640,4096]{1,0:T(8,128)(2,1)}, bf16[4096,640]{1,0:T(8,128)(2,1)}, bf16[640,4096]{1,0:T(8,128)(2,1)}, bf16[640,4096]{1,0:T(8,128)(2,1)}, bf16[6...) custom-call(bf16[4096,640]{1,0:T(8,128)(2,1)} %bitcast.4, bf16[4096,640]{1,0:T(8,128)(2,1)} %bitcast.2, ...), custom_call_target="tpu_custom_call" | custom-call | tf_op jit(solution)/shard_map/forward/pallas_call | solution.py:121
  43.4 92.9 %backward1.1 = (bf16[2,160,512]{2,1,0:T(8,128)(2,1)}, bf16[128,640]{1,0:T(8,128)(2,1)}, f32[8,128]{1,0:T(8,128)}, bf16[2,160,512]{2,1,0:T(8,128)(2,1)}, bf16[128...) custom-call(bf16[640,4096]{1,0:T(8,128)(2,1)} %get-tuple-element.46.refs_0_, ...), custom_call_target="tpu_custom_call" | custom-call | tf_op jit(solution)/shard_map/backward1/pallas_call | solution.py:445
  136.3 65.7 %backward0.1 = (bf16[2,160,512]{2,1,0:T(8,128)(2,1)}, bf16[128,640]{1,0:T(8,128)(2,1)}, f32[8,128]{1,0:T(8,128)}, bf16[2,160,512]{2,1,0:T(8,128)(2,1)}, bf16[128...) custom-call(bf16[640,4096]{1,0:T(8,128)(2,1)} %get-tuple-element.43., ...), custom_call_target="tpu_custom_call" | custom-call | tf_op jit(solution)/shard_map/backward0/pallas_call | solution.py:445
  202.0 124.9 %update.1 = (bf16[2,640,1536]{2,1,0:T(8,128)(2,1)S(1)}, bf16[2,640,1536]{2,1,0:T(8,128)(2,1)S(1)}, bf16[2,1536,640]{2,1,0:T(8,128)(2,1)S(1)}, f32[2,160,1536]{2,...) custom-call(bf16[4,2,240,512]{3,2,1,0:T(8,128)(2,1)} %get-tuple-elem, ...), custom_call_target="tpu_custom_call" | custom-call | tf_op jit(solution)/shard_map/update/pallas_call | solution.py:607
  326.8 8.1 %put.1 = (bf16[2,640,1536]{2,1,0:T(8,128)(2,1)}, bf16[2,640,1536]{2,1,0:T(8,128)(2,1)}, bf16[2,1536,640]{2,1,0:T(8,128)(2,1)}, f32[2,160,1536]{2,1,0:T(8,128)}, ...) custom-call(bf16[2,640,1536]{2,1,0:T(8,128)(2,1)S(1)} %get-tuple-ele, ...), custom_call_target="tpu_custom_call" | custom-call | tf_op jit(solution)/shard_map/put/pallas_call | solution.py:647

commit v3 on v2

v3 whole, which is shorter than its diff:
```python
import functools

import jax
import jax.numpy as jnp
from jax import lax
from jax.experimental import pallas as pl
from jax.experimental.pallas import tpu as pltpu
from jax.sharding import PartitionSpec as P

F32, BF16 = jnp.float32, jnp.bfloat16
LANES = 128
AXIS = "dp"
MESH = pl.DeviceIdType.MESH
VMEM_LIMIT = 64 * 1024 * 1024 - 192 * 1024
VMEM, RESERVE = 64 * 1024 * 1024, 192 * 1024
SUB = 256
SUB_BACK = 512
ROWS, COLS = (((0,), (0,)), ((), ())), (((1,), (1,)), ((), ()))


def dot(a, b):
    return jnp.dot(a, b, preferred_element_type=F32)


def dot_t(a, b):
    return lax.dot_general(a, b, COLS, preferred_element_type=F32)


def sigmoid(g):
    return 0.5 * jnp.tanh(0.5 * g) + 0.5


def normed(wide, axis):
    scale = lax.rsqrt(jnp.mean(wide * wide, axis, keepdims=True) + 1e-6)
    return (wide * scale).astype(BF16)


def greet(peers):
    barrier = pltpu.get_barrier_semaphore()
    for peer in peers:
        pl.semaphore_signal(barrier, inc=1, device_id={AXIS: peer}, device_id_type=MESH)
    pl.semaphore_wait(barrier, len(peers))


def fetch(w_refs, layer, n, chunk, buffers, sems):
    copies = []
    for k, (w, buffer) in enumerate(zip(w_refs, buffers)):
        if buffer is None:
            continue
        own = w.shape[1 if k == 2 else 2] // n
        for o in range(n):
            there = pl.ds(pl.multiple_of(o * own + chunk * LANES, LANES), LANES)
            here = pl.ds(o * LANES, LANES)
            if k == 2:
                copies.append(pltpu.make_async_copy(w.at[layer, there, :], buffer.at[here, :], sems.at[k, o]))
            else:
                copies.append(pltpu.make_async_copy(w.at[layer, :, there], buffer.at[:, here], sems.at[k, o]))
    return copies


def forward_kernel(n, layer, early, x_ref, dy_ref, wg_ref, wu_ref, wd_ref, mg_ref, mu_ref, vg_ref, vu_ref, a1t_ref, a2_ref, a2t_ref, h1t_ref, dyt_ref, gate_ref, up_ref, near_ref, wg, wu, wd, w_sem, near_send, near_recv):
    chunks = wg.shape[0]
    parts = x_ref.shape[0] // SUB

    def weights(c):
        return fetch((wg_ref, wu_ref, wd_ref), layer, n, c, (wg.at[c], wu.at[c], wd.at[c]), w_sem.at[c])

    def moments():
        me = lax.axis_index(AXIS)
        own = mg_ref.shape[2] // n
        for side, to in enumerate(((me + 1) % n, (me + n - 1) % n)):
            for j, pair in enumerate(((mg_ref, mu_ref), (vg_ref, vu_ref))):
                for k, source in enumerate(pair):
                    for o in range(n):
                        yield pltpu.make_async_remote_copy(
                            src_ref=source.at[early, :, pl.ds(o * own, LANES)],
                            dst_ref=near_ref.at[side, j, k, :, pl.ds(o * LANES, LANES)],
                            send_sem=near_send.at[side, j, k, o],
                            recv_sem=near_recv.at[side, j, k, o],
                            device_id={AXIS: to},
                            device_id_type=MESH,
                        )

    @pl.when(pl.program_id(0) == 0)
    def _():
        for c in range(chunks):
            for copy in weights(c):
                copy.start()
        me = lax.axis_index(AXIS)
        greet(((me + n - 1) % n, (me + 1) % n))
        for copy in moments():
            copy.start()
        for c in range(chunks):
            for copy in weights(c):
                copy.wait()

    def before(p):
        here = slice(p * SUB, (p + 1) * SUB)
        a1 = normed(x_ref[here, :].astype(F32), -1)
        a1t_ref[:, here] = a1.T
        dyt_ref[:, here] = dy_ref[here, :].T
        return a1

    def first(p, a1, c):
        here = slice(p * SUB, (p + 1) * SUB)
        gate, up = dot(a1, wg[c]), dot(a1, wu[c])
        gate_ref[c, here, :] = gate
        up_ref[c, here, :] = up
        return gate, up

    def after(p, down):
        here = slice(p * SUB, (p + 1) * SUB)
        h1 = (x_ref[here, :].astype(F32) + down.astype(BF16).astype(F32)).astype(BF16)
        h1t_ref[:, here] = h1.T
        a2 = normed(h1.astype(F32), -1)
        a2_ref[here, :] = a2
        a2t_ref[:, here] = a2.T

    todo = [(p, c) for p in range(parts) for c in range(chunks)]
    a1 = before(0)
    ahead, down = first(0, a1, 0), None
    for i, (p, c) in enumerate(todo):
        gate, up = ahead
        if i + 1 < len(todo):
            q, e = todo[i + 1]
            if q != p:
                a1 = before(q)
            ahead = first(q, a1, e)
        hidden = (gate * sigmoid(gate) * up).astype(BF16)
        term = dot(hidden, wd[c])
        down = term if c == 0 else down + term
        if c + 1 == chunks:
            after(p, down)

    @pl.when(pl.program_id(0) == pl.num_programs(0) - 1)
    def _():
        for copy in moments():
            copy.wait()


def forward(n, x, dy, w, moments, layer, early, tile=512, collective_id=3):
    tokens, d = x.shape
    ff = w[0].shape[-1]
    width = n * LANES
    chunks = ff // width
    rows = pl.BlockSpec((tile, d), lambda t: (t, 0))
    columns = pl.BlockSpec((d, tile), lambda t: (0, t))
    inside = pl.BlockSpec((chunks, tile, width), lambda t: (0, t, 0))
    weight = pl.BlockSpec(memory_space=pltpu.HBM)
    straight, turned = jax.ShapeDtypeStruct((tokens, d), BF16), jax.ShapeDtypeStruct((d, tokens), BF16)
    kept = jax.ShapeDtypeStruct((chunks, tokens, width), F32)
    return pl.pallas_call(
        functools.partial(forward_kernel, n, layer, early),
        grid=(tokens // tile,),
        in_specs=[rows, rows, *[weight] * 7],
        out_specs=[columns, rows, columns, columns, columns, inside, inside, weight],
        out_shape=[turned, straight, turned, turned, turned, kept, kept, jax.ShapeDtypeStruct((2, 2, 2, d // n, width), F32)],
        scratch_shapes=[
            pltpu.VMEM((chunks, d, width), BF16),
            pltpu.VMEM((chunks, d, width), BF16),
            pltpu.VMEM((chunks, width, d), BF16),
            pltpu.SemaphoreType.DMA((chunks, 3, n)),
            pltpu.SemaphoreType.DMA((2, 2, 2, n)),
            pltpu.SemaphoreType.DMA((2, 2, 2, n)),
        ],
        compiler_params=pltpu.CompilerParams(vmem_limit_bytes=VMEM_LIMIT, collective_id=collective_id, has_side_effects=True),
        name="forward",
    )(x, dy, *w, *moments)


class Ring:
    def __init__(self, n, recv, summed, send_sem, recv_sem):
        self.me = lax.axis_index(AXIS)
        self.n, self.recv, self.summed, self.send_sem, self.recv_sem = n, recv, summed, send_sem, recv_sem
        self.right, self.left = (self.me + 1) % n, (self.me + n - 1) % n
        self.part = recv.shape[2] // 3

    def rows(self, s):
        return pl.ds(s * self.part, self.part)

    def hop(self, i, s, k, blocks):
        far, rows = (self.me + 2) % self.n, self.rows(s)
        if k >= 4:
            src = self.summed.at[i, k - 4, rows]
        else:
            src = blocks.at[(far, far, self.right, self.left)[k], (0, 1, 1, 0)[k], rows]
        return pltpu.make_async_remote_copy(
            src_ref=src,
            dst_ref=self.recv.at[i, k, rows],
            send_sem=self.send_sem.at[i, s, k],
            recv_sem=self.recv_sem.at[i, s, k],
            device_id={AXIS: (self.right, self.left)[k % 2]},
            device_id_type=MESH,
        )

    def start(self, i, blocks, parts=(0, 1, 2)):
        for k in ((0, 1), (2, 3)):
            for s in parts:
                for one in k:
                    self.hop(i, s, one, blocks).start()

    def pass_on(self, i, blocks, parts=(0, 1, 2)):
        for s in parts:
            rows = self.rows(s)
            for k, to in enumerate((self.right, self.left)):
                self.hop(i, s, k, blocks).wait_recv()
                self.summed[i, k, rows] = (blocks[to, k, rows].astype(F32) + self.recv[i, k, rows].astype(F32)).astype(BF16)
                self.hop(i, s, 4 + k, blocks).start()

    def finish(self, i, blocks):
        for s in range(3):
            for k in range(6):
                hop = self.hop(i, s, k, blocks)
                if k >= 2:
                    hop.wait_recv()
                hop.wait_send()
        me = self.me
        return [
            (blocks[me, half].astype(F32) + self.recv[i, 4 + half].astype(F32) + self.recv[i, 3 - half].astype(F32)).astype(BF16)
            for half in range(2)
        ]


def pack(blocks, n, s, acc):
    half = acc.shape[0] // n // 2
    for o in range(n):
        for h in range(2):
            if s < 2:
                blocks[o, h, s * half : (s + 1) * half, :] = acc[(2 * o + h) * half : (2 * o + h + 1) * half, :].astype(BF16)
                continue
            for b in range(n):
                blocks[o, h, s * half : (s + 1) * half, b * LANES : (b + 1) * LANES] = acc[
                    (h * n + b) * half : (h * n + b + 1) * half, o * LANES : (o + 1) * LANES
                ].astype(BF16)


def unpack(halves, n, gu_ref, d_ref, ss_ref):
    half = halves[0].shape[0] // 3
    squares = jnp.zeros(ss_ref.shape, F32)
    for h, block in enumerate(halves):
        gu_ref[0, h * half : (h + 1) * half, :] = block[0:half]
        gu_ref[1, h * half : (h + 1) * half, :] = block[half : 2 * half]
        wide = block.astype(F32)
        s = jnp.sum((wide * wide).reshape(-1, 8, wide.shape[1]), axis=0)
        for b in range(n):
            squares = squares + s[:, b * LANES : (b + 1) * LANES]
            d_ref[:, (h * n + b) * half : (h * n + b + 1) * half] = block[2 * half :, b * LANES : (b + 1) * LANES].astype(F32).T.astype(BF16)
    ss_ref[...] = squares


def through(gate, up, dhidden):
    dhidden = dhidden.astype(BF16).astype(F32)
    s = sigmoid(gate)
    silu = gate * s
    return (silu * up).astype(BF16), (dhidden * silu).astype(BF16), (dhidden * up * (s + silu * (1 - s))).astype(BF16)


def prefetch(weights, chunks, c, t):
    slot = c % 2

    @pl.when((c == 0) & (t == 0))
    def _():
        for copy in weights(0, 0):
            copy.start()

    @pl.when(t == 0)
    def _():
        for copy in weights(c, slot):
            copy.wait()

    @pl.when((t == 0) & (c < chunks - 1))
    def _():
        for copy in weights(c + 1, 1 - slot):
            copy.start()

    return slot


def inner_kernel(n, chunks, tiles, layer, *refs):
    refs = list(refs)
    take = lambda count: [refs.pop(0) for _ in range(count)]
    at_ref, a_ref, dy_ref, dyt_ref = take(4)
    w_refs = take(3)
    near_ref = take(1)[0]
    outs = take(3)
    last_ref, dat_out, far_ref, early_ref = take(4)
    acc_g, acc_u, acc_d, blocks, recv, summed, send_sem, recv_sem = take(8)
    wd_now, w_sem, wg_now, wu_now, dat_ref, dat_kept, dat_sem, mine_ref, early_send, early_recv = take(10)

    c, t = pl.program_id(0), pl.program_id(1)
    tile = a_ref.shape[0]
    ring = Ring(n, recv, summed, send_sem, recv_sem)

    def send(k, src, dst):
        return pltpu.make_async_remote_copy(
            src_ref=src,
            dst_ref=dst,
            send_sem=early_send.at[k],
            recv_sem=early_recv.at[k],
            device_id={AXIS: (ring.right, ring.left)[k % 2]},
            device_id_type=MESH,
        )

    def onward():
        return [send(k, near_ref.at[k, k], far_ref.at[k]) for k in range(2)]

    def spread():
        return [send(2 + k, mine_ref, early_ref.at[k]) for k in range(2)]

    def spread_on():
        return [send(4 + k, early_ref.at[k, k], early_ref.at[2, k]) for k in range(2)]

    @pl.when((c == 0) & (t == 0))
    def _():
        greet((ring.left, ring.right))
        for copy in onward():
            copy.start()

    @pl.when((c == 0) & (t == tiles - 1))
    def _():
        for copy in onward():
            copy.wait()

    def weights(chunk, slot):
        return fetch(w_refs, layer, n, chunk, [now.at[slot] for now in (wg_now, wu_now, wd_now)], w_sem.at[slot])

    slot = prefetch(weights, chunks, c, t)
    wg, wu, wd = wg_now.at[slot], wu_now.at[slot], wd_now.at[slot]
    accs = acc_g, acc_u, acc_d

    @pl.when(t == 0)
    def _():
        for acc in accs:
            acc[...] = jnp.zeros_like(acc)

    @pl.when(c == 0)
    def _():
        dat_ref[:, pl.ds(pl.multiple_of(t * tile, tile), tile)] = jnp.zeros((dat_ref.shape[0], tile), F32)

    def first(p):
        rows = slice(p * SUB_BACK, (p + 1) * SUB_BACK)
        a = a_ref[rows, :]
        return dot(a, wg[...]), dot(a, wu[...]), dot_t(dy_ref[rows, :], wd[...])

    def second(p, hidden, dup, dgate):
        columns = slice(p * SUB_BACK, (p + 1) * SUB_BACK)
        here = pl.ds(pl.multiple_of(t * tile + p * SUB_BACK, SUB_BACK), SUB_BACK)
        dat_ref[:, here] += dot_t(wg[...], dgate) + dot_t(wu[...], dup)
        at = at_ref[:, columns]
        acc_g[...] += dot(at, dgate)
        acc_u[...] += dot(at, dup)
        acc_d[...] += dot(dyt_ref[:, columns], hidden)

    parts = tile // SUB_BACK
    ahead = first(0)
    for p in range(parts):
        now = ahead
        if p + 1 < parts:
            ahead = first(p + 1)
        second(p, *through(*now))

    def keep(tile_number):
        here = pl.ds(pl.multiple_of(tile_number * tile, tile), tile)
        return pltpu.make_async_copy(dat_kept, dat_out.at[:, here], dat_sem.at[tile_number])

    @pl.when((c == chunks - 1) & (t > 0))
    def _():
        keep(t - 1).wait()

    @pl.when(c == chunks - 1)
    def _():
        dat_kept[...] = dat_ref[:, pl.ds(pl.multiple_of(t * tile, tile), tile)].astype(BF16)
        keep(t).start()

    @pl.when((c == chunks - 1) & (t == tiles - 1))
    def _():
        keep(t).wait()

    def end(i):
        unpack(ring.finish(i, blocks.at[i]), n, *[out.at[i] for out in outs])

    @pl.when((c > 0) & (t == 0))
    def _():
        ring.pass_on(c - 1, blocks.at[c - 1])

    @pl.when((c == 2) & (t == 0))
    def _():
        for copy in spread():
            copy.wait_recv()
        for copy in spread_on():
            copy.start()

    @pl.when((c > 0) & (t == tiles - 1))
    def _():
        end(c - 1)

    @pl.when((c == 1) & (t == tiles - 1))
    def _():
        for k in range(2):
            for h in range(2):
                mine_ref[h, k] = outs[0][0, k, h * mine_ref.shape[2] : (h + 1) * mine_ref.shape[2], :]
        for copy in spread():
            copy.start()

    @pl.when((c == chunks - 1) & (t == tiles - 1))
    def _():
        for copy in spread():
            copy.wait_send()
        for copy in spread_on():
            copy.wait()

    @pl.when((c < chunks - 1) & (t == tiles - 1))
    def _():
        for s in range(3):
            pack(blocks.at[c], n, s, accs[s])
        ring.start(c, blocks.at[c])

    @pl.when((c == chunks - 1) & (t == tiles - 1))
    def _():
        for s in range(3):
            pack(last_ref, n, s, accs[s])


def outer_kernel(n, chunks, tiles, layer, *refs):
    refs = list(refs)
    take = lambda count: [refs.pop(0) for _ in range(count)]
    at_in, gate_ref, up_ref, dat_ref, h1t_ref, dyt_ref = take(6)
    w_refs = take(3)
    carried_ref = take(1)[0]
    outs = take(3)
    acc, acc_g, blocks, recv, summed, send_sem, recv_sem = take(7)
    wd_now, w_sem, at_ref, at_sem, dh_ref, dht_ref, dup_ref, carried_sem = take(8)

    c, t = pl.program_id(0), pl.program_id(1)
    tile = gate_ref.shape[0]
    ring = Ring(n, recv, summed, send_sem, recv_sem)
    whole = pltpu.make_async_copy(at_in, at_ref, at_sem)

    @pl.when((c == 0) & (t == 0))
    def _():
        carried = pltpu.make_async_copy(carried_ref, blocks.at[0], carried_sem)
        carried.start()
        whole.start()
        greet((ring.left, ring.right))
        carried.wait()
        ring.start(0, blocks.at[0])

    def weights(chunk, slot):
        return fetch(w_refs, layer, n, chunk, [None, None, wd_now.at[slot]], w_sem.at[slot])

    wd = wd_now.at[prefetch(weights, chunks, c, t)]

    @pl.when(t == 0)
    def _():
        acc[...] = jnp.zeros_like(acc)
        acc_g[...] = jnp.zeros_like(acc_g)

    @pl.when((c == 0) & (t < tiles))
    def _():
        width = 2 * LANES
        for p in range(tile // width):
            here = slice(p * width, (p + 1) * width)
            there = pl.ds(pl.multiple_of(t * tile + p * width, width), width)
            da = dat_ref[:, here].astype(F32)
            wide = h1t_ref[:, here].astype(F32)
            scale = lax.rsqrt(jnp.mean(wide * wide, 0, keepdims=True) + 1e-6)
            along = jnp.mean(da * wide, 0, keepdims=True)
            dwide = da * scale - wide * (scale * scale * scale * along)
            dht = (dyt_ref[:, here].astype(F32) + dwide.astype(BF16).astype(F32)).astype(BF16)
            dht_ref[:, there] = dht
            dh_ref[there, :] = dht.T

    @pl.when((c == 0) & (t == 0))
    def _():
        whole.wait()

    @pl.when(t < tiles)
    def _():
        def place(p):
            return pl.ds(pl.multiple_of(t * tile + p * SUB_BACK, SUB_BACK), SUB_BACK)

        def first(p):
            rows = slice(p * SUB_BACK, (p + 1) * SUB_BACK)
            return gate_ref[rows, :], up_ref[rows, :], dot_t(dh_ref[place(p), :], wd[...])

        parts = tile // SUB_BACK
        ahead = first(0)
        for p in range(parts):
            now = ahead
            if p + 1 < parts:
                ahead = first(p + 1)
            hidden, dup, dgate = through(*now)
            dup_ref[place(p), :] = dup
            acc[...] += dot(dht_ref[:, place(p)], hidden)
            acc_g[...] += dot(at_ref[:, place(p)], dgate)

    def end(i):
        unpack(ring.finish(i, blocks.at[i]), n, *[out.at[i] for out in outs])

    @pl.when((c == 0) & (t == 1))
    def _():
        ring.pass_on(0, blocks.at[0])

    @pl.when((c > 0) & (t == 0))
    def _():
        ring.pass_on(c, blocks.at[c], (2, 0))

    @pl.when((c > 0) & (t == 2))
    def _():
        ring.pass_on(c, blocks.at[c], (1,))

    i = c + 1
    here = blocks.at[i]

    @pl.when(t == tiles - 1)
    def _():
        pack(here, n, 2, acc)
        pack(here, n, 0, acc_g)
        ring.start(i, here, (2, 0))

    @pl.when(t == tiles)
    def _():
        acc[...] = dot(at_ref[...], dup_ref[...])
        pack(here, n, 1, acc)
        ring.start(i, here, (1,))
        end(c)

    @pl.when((c == chunks - 1) & (t == tiles))
    def _():
        ring.pass_on(i, here, (2, 0, 1))
        end(i)


def sizes(n, w):
    d, ff = w[0].shape[1:]
    width, rows = n * LANES, 3 * (d // n // 2)
    return d, width, ff // width, (n, 2, rows, width)


def sums_of(count, d, n, width):
    shapes = ((count, 2, d // n, width), BF16), ((count, LANES, d), BF16), ((count, 8, LANES), F32)
    return [once(shape) for shape, _ in shapes], [jax.ShapeDtypeStruct(*one) for one in shapes]


def ring_scratch(count, packed):
    _, _, rows, width = packed
    return [
        pltpu.VMEM((count, 6, rows, width), BF16),
        pltpu.VMEM((count, 2, rows, width), BF16),
        pltpu.SemaphoreType.DMA((count, 3, 6)),
        pltpu.SemaphoreType.DMA((count, 3, 6)),
    ]


def once(shape):
    return pl.BlockSpec(shape, lambda c, t: (0,) * len(shape), pipeline_mode=pl.Buffered(1))


HBM = pl.BlockSpec(memory_space=pltpu.HBM)


def backward_inner(n, at, a, dy, dyt, w, near, layer, tile=2048, collective_id=0):
    tokens = at.shape[1]
    d, width, chunks, packed = sizes(n, w)
    tiles = tokens // tile
    straight = pl.BlockSpec((tile, d), lambda c, t: (t, 0))
    turned = pl.BlockSpec((d, tile), lambda c, t: (0, t))
    specs, shapes = sums_of(chunks - 1, d, n, width)
    early = (3, 2, 2, d // n // 2, width)
    *sums, last, dat, far, gradients = pl.pallas_call(
        functools.partial(inner_kernel, n, chunks, tiles, layer),
        grid=(chunks, tiles),
        in_specs=[turned, straight, straight, turned, HBM, HBM, HBM, HBM],
        out_specs=[*specs, once(packed), HBM, HBM, HBM],
        out_shape=[
            *shapes,
            jax.ShapeDtypeStruct(packed, BF16),
            jax.ShapeDtypeStruct((d, tokens), BF16),
            jax.ShapeDtypeStruct(near.shape[1:], F32),
            jax.ShapeDtypeStruct(early, BF16),
        ],
        scratch_shapes=[
            *[pltpu.VMEM((d, width), F32)] * 3,
            pltpu.VMEM((chunks - 1, *packed), BF16),
            *ring_scratch(chunks - 1, packed),
            pltpu.VMEM((2, width, d), BF16),
            pltpu.SemaphoreType.DMA((2, 3, n)),
            pltpu.VMEM((2, d, width), BF16),
            pltpu.VMEM((2, d, width), BF16),
            pltpu.VMEM((d, tokens), F32),
            pltpu.VMEM((d, tile), BF16),
            pltpu.SemaphoreType.DMA((tiles,)),
            pltpu.VMEM(early[1:], BF16),
            pltpu.SemaphoreType.DMA((6,)),
            pltpu.SemaphoreType.DMA((6,)),
        ],
        compiler_params=pltpu.CompilerParams(
            vmem_limit_bytes=VMEM_LIMIT, collective_id=collective_id, has_side_effects=True,
            dimension_semantics=("arbitrary", "arbitrary"),
        ),
        name="backward_inner",
    )(at, a, dy, dyt, *w, near)
    return sums, last, dat, far, gradients


def backward_outer(n, at, gate, up, dat, h1t, dyt, w, layer, carried, tile=1024, collective_id=1):
    tokens = at.shape[1]
    d, width, chunks, packed = sizes(n, w)
    tiles = tokens // tile
    at_first = pl.BlockSpec((d, tile), lambda c, t: (0, jnp.where(c == 0, jnp.minimum(t, tiles - 1), tiles - 1)))
    inside = pl.BlockSpec((None, tile, width), lambda c, t: (c, jnp.minimum(t, tiles - 1), 0))
    specs, shapes = sums_of(chunks + 1, d, n, width)
    return pl.pallas_call(
        functools.partial(outer_kernel, n, chunks, tiles, layer),
        grid=(chunks, tiles + 1),
        in_specs=[HBM, inside, inside, at_first, at_first, at_first, HBM, HBM, HBM, HBM],
        out_specs=specs,
        out_shape=shapes,
        scratch_shapes=[
            pltpu.VMEM((d, width), F32),
            pltpu.VMEM((d, width), F32),
            pltpu.VMEM((chunks + 1, *packed), BF16),
            *ring_scratch(chunks + 1, packed),
            pltpu.VMEM((2, width, d), BF16),
            pltpu.SemaphoreType.DMA((2, 3, n)),
            pltpu.VMEM((d, tokens), BF16),
            pltpu.SemaphoreType.DMA,
            pltpu.VMEM((tokens, d), BF16),
            pltpu.VMEM((d, tokens), BF16),
            pltpu.VMEM((tokens, width), BF16),
            pltpu.SemaphoreType.DMA,
        ],
        compiler_params=pltpu.CompilerParams(
            vmem_limit_bytes=VMEM_LIMIT, collective_id=collective_id, has_side_effects=True,
            dimension_semantics=("arbitrary", "arbitrary"),
        ),
        name="backward_outer",
    )(at, gate, up, dat, h1t, dyt, *w, carried)


def update_kernel(n, chunks, layers, count, *refs):
    refs = list(refs)
    take = lambda k: [refs.pop(0) for _ in range(k)]
    many = layers * chunks
    sums_in = [take(3), take(3)]
    near_in, far_in, early_in = take(3)
    w_in, m_in, v_in = take(3), take(3), take(3)
    w_out, m_own, v_own = take(3), take(3), take(3)
    gu_all, gd_all, squares = take(3)
    w_own = take(3)
    ss_mine, ss_all, ss_send, ss_recv = take(4)
    load_sem, sums_sem, gather_send, gather_recv = take(4)
    near, far, early, w_early, early_sem, w_sem = take(6)

    me = lax.axis_index(AXIS)
    right, left = (me + 1) % n, (me + n - 1) % n
    own_rows = [m.shape[1] for m in m_own]

    def mine(k, owner, h=None):
        rows = own_rows[k]
        if h is None:
            return pl.ds(pl.multiple_of(owner * rows, 16), rows)
        return pl.ds(pl.multiple_of(owner * rows + h * (rows // 2), 16), rows // 2)

    loads = []
    for k in range(3):
        for l in range(layers):
            i = len(loads)
            loads.append(
                (
                    pltpu.make_async_copy(w_in[k].at[l, mine(k, me)], w_own[k].at[l], load_sem.at[0, k, l]),
                    pltpu.make_async_copy(m_in[k].at[l], m_own[k].at[l], load_sem.at[1, k, l]),
                    pltpu.make_async_copy(v_in[k].at[l], v_own[k].at[l], load_sem.at[2, k, l]),
                )
            )
    sum_loads, done = [], 0
    for i, one in enumerate(sums_in):
        count_here = one[0].shape[0]
        for j, (src, dst) in enumerate(zip(one, (gu_all, gd_all, squares))):
            sum_loads.append(pltpu.make_async_copy(src, dst.at[pl.ds(done, count_here)], sums_sem.at[i, j]))
        done += count_here
    for copy in sum_loads:
        copy.start()
    for load in loads:
        for copy in load:
            copy.start()
    own = w_in[0].shape[2] // n
    other_loads = [
        pltpu.make_async_copy(src, dst, early_sem.at[i])
        for i, (src, dst) in enumerate(((near_in, near), (far_in, far), (early_in, early)))
    ]
    for k in range(2):
        for o in range(n):
            there = pl.ds(o * own, LANES)
            other_loads.append(
                pltpu.make_async_copy(w_in[k].at[layers - 1, :, there], w_early.at[k, :, pl.ds(o * LANES, LANES)], w_sem.at[k, o])
            )
    for copy in other_loads:
        copy.start()
    peers = [(me + i) % n for i in range(1, n)]
    greet(peers)
    for copy in sum_loads:
        copy.wait()

    total = squares[0]
    for i in range(1, many):
        total = total + squares[i]
    ss_mine[...] = total
    shares = [
        pltpu.make_async_remote_copy(
            src_ref=ss_mine, dst_ref=ss_all.at[i], send_sem=ss_send.at[i], recv_sem=ss_recv.at[i],
            device_id={AXIS: peer}, device_id_type=MESH,
        )
        for i, peer in enumerate(peers)
    ]
    for share in shares:
        share.start()
    for share in shares:
        share.wait()
    for i in range(n - 1):
        total = total + ss_all[i]
    mean = jnp.sum(jnp.sum(total, axis=0, keepdims=True), axis=1, keepdims=True) / count
    factor = jnp.minimum(1.0, 0.5 * lax.rsqrt(mean + 1e-30))

    def gather(k, l, owner, h, way, to):
        rows = mine(k, owner, h)
        if l == layers - 1 and k < 2:
            places = [(rows, pl.ds(o * own + LANES, own - LANES)) for o in range(n)]
        else:
            places = [(rows, slice(None))]
        return [
            pltpu.make_async_remote_copy(
                src_ref=w_out[k].at[l, *place],
                dst_ref=w_out[k].at[l, *place],
                send_sem=gather_send.at[k, l, h, way, i],
                recv_sem=gather_recv.at[k, l, h, way, i],
                device_id={AXIS: to},
                device_id_type=MESH,
            )
            for i, place in enumerate(places)
        ]

    def own_send(k, l, h, way):
        return gather(k, l, me, h, way, (right, left)[way])

    def onward(k, l, way):
        owner, to = ((left, right), (right, left))[way]
        return gather(k, l, owner, way, 2, to)

    def adamw(w, m, v, g):
        w, g = w.astype(F32), g.astype(F32) * factor
        m = 0.9 * m + 0.1 * g
        v = 0.95 * v + 0.05 * g * g
        return (w - 0.02 * (m * lax.rsqrt(v + 1e-8) + 0.1 * w)).astype(BF16), m, v

    order = [(k, l) for l in reversed(range(layers)) for k in range(3)]
    for k, l in order:
        for copy in loads[k * layers + l]:
            copy.wait()
        base = (layers - 1 - l) * chunks

        def step(rows, columns, g):
            there = pl.ds(pl.multiple_of(me * own_rows[k] + rows.start, 16), rows.stop - rows.start)
            w_out[k][l, there, columns], m, v = adamw(w_own[k][l, rows, columns], m_own[k][l, rows, columns], v_own[k][l, rows, columns], g)
            m_own[k][l, rows, columns] = m
            v_own[k][l, rows, columns] = v

        for c in range(chunks):
            if k == 2:
                step(slice(c * LANES, (c + 1) * LANES), slice(None), gd_all[base + c])
            else:
                for o in range(n):
                    at = o * chunks * LANES + c * LANES
                    step(slice(0, own_rows[k]), slice(at, at + LANES), gu_all[base + c, k, :, o * LANES : (o + 1) * LANES])
        for h in range(2):
            for way in range(2):
                for copy in own_send(k, l, (h + way) % 2, way):
                    copy.start()
    for copy in other_loads:
        copy.wait()
    half = own_rows[0] // 2
    for r, owner in enumerate((left, right, (me + 2) % n)):
        for k in range(2):
            for h in range(2):
                rows, there = slice(h * half, (h + 1) * half), mine(k, owner, h)
                for o in range(n):
                    columns = slice(o * LANES, (o + 1) * LANES)
                    m, v = (near[r, j, k, rows, columns] if r < 2 else far[j, k, rows, columns] for j in range(2))
                    new, _, _ = adamw(w_early[k, there, columns], m, v, early[r, h, k, :, columns])
                    w_out[k][layers - 1, there, o * own : o * own + LANES] = new
    for k, l in order:
        for way in range(2):
            for copy in own_send(k, l, way, way):
                copy.wait_recv()
            for copy in onward(k, l, way):
                copy.start()
    for k, l in order:
        for way in range(2):
            for copy in own_send(k, l, 1 - way, way):
                copy.wait_recv()
            for copy in onward(k, l, way):
                copy.wait_recv()
                copy.wait_send()
            for h in range(2):
                for copy in own_send(k, l, h, way):
                    copy.wait_send()


def update(n, sums, others, w, m, v, collective_id):
    layers = w[0].shape[0]
    chunks = w[0].shape[2] // n // LANES
    count = sum(t.size for t in w)
    width = n * LANES
    vmem = pl.BlockSpec(memory_space=pltpu.VMEM)
    own = [t.shape for t in m]
    many = layers * chunks
    return pl.pallas_call(
        functools.partial(update_kernel, n, chunks, layers, count),
        in_specs=[HBM] * (len(sums) + 12),
        out_specs=[vmem] * 9,
        out_shape=[pltpu.VMEM(t.shape, t.dtype) for t in (*w, *m, *v)],
        scratch_shapes=[
            pltpu.VMEM((many, 2, w[0].shape[1] // n, width), BF16),
            pltpu.VMEM((many, LANES, w[0].shape[1]), BF16),
            pltpu.VMEM((many, 8, LANES), F32),
            *[pltpu.VMEM(s, BF16) for s in own],
            pltpu.VMEM((8, LANES), F32),
            pltpu.VMEM((n - 1, 8, LANES), F32),
            pltpu.SemaphoreType.DMA((n - 1,)),
            pltpu.SemaphoreType.DMA((n - 1,)),
            pltpu.SemaphoreType.DMA((3, 3, layers)),
            pltpu.SemaphoreType.DMA((2, 3)),
            pltpu.SemaphoreType.DMA((3, layers, 2, 3, n)),
            pltpu.SemaphoreType.DMA((3, layers, 2, 3, n)),
            *[pltpu.VMEM(t.shape, t.dtype) for t in others],
            pltpu.VMEM((2, w[0].shape[1], width), BF16),
            pltpu.SemaphoreType.DMA((3,)),
            pltpu.SemaphoreType.DMA((2, n)),
        ],
        compiler_params=pltpu.CompilerParams(vmem_limit_bytes=VMEM - RESERVE - sum(t.size * t.dtype.itemsize for t in (*w, *m, *v)), collective_id=collective_id, has_side_effects=True),
        name="update",
    )(*sums, *others, *w, *m, *v)


def put_kernel(count, *refs):
    sources, targets, sem = refs[:count], refs[count : 2 * count], refs[2 * count]
    copies = [pltpu.make_async_copy(a, b, sem.at[i]) for i, (a, b) in enumerate(zip(sources, targets))]
    for copy in copies:
        copy.start()
    for copy in copies:
        copy.wait()


def put(arrays):
    return pl.pallas_call(
        functools.partial(put_kernel, len(arrays)),
        in_specs=[pl.BlockSpec(memory_space=pltpu.VMEM)] * len(arrays),
        out_specs=[pl.BlockSpec(memory_space=pltpu.HBM)] * len(arrays),
        out_shape=[jax.ShapeDtypeStruct(t.shape, t.dtype) for t in arrays],
        scratch_shapes=[pltpu.SemaphoreType.DMA((len(arrays),))],
        compiler_params=pltpu.CompilerParams(vmem_limit_bytes=16 * 1024 * 1024),
        name="put",
    )(*arrays)


def solution(mesh):
    n = mesh.shape[AXIS]

    def step(x, dy, *arrays):
        w, m, v = arrays[:3], arrays[3:6], arrays[6:9]
        x, dy = x.reshape(x.shape[-2:]), dy.reshape(dy.shape[-2:])
        a1t, a2, a2t, h1t, dyt, *kept, near = forward(n, x, dy, w, (*m[:2], *v[:2]), 0, 1)
        sums2, last2, dat, far, early = backward_inner(n, a2t, a2, dy, dyt, w, near, 1)
        sums1 = backward_outer(n, a1t, *kept, dat, h1t, dyt, w, 0, last2)
        return tuple(put(update(n, [*sums2, *sums1], (near, far, early), w, m, v, 2)))

    whole, rows = P(None, None, None), P(None, AXIS, None)
    own, own_rows = P("rep", None, None), P("rep", AXIS, None)
    one = P(("rep", AXIS), None, None)
    return jax.shard_map(
        step,
        mesh=mesh,
        in_specs=(one, one, *[whole] * 3, *[rows] * 6),
        out_specs=(*[own] * 3, *[own_rows] * 6),
        check_vma=False,
    )
```

time: 335 us -> 325 us (0.970)
  Pallas kernels: 334 us -> 324 us
    pallas_call x1, Pallas kernels: 125 us -> 98.4 us  [update(): pl.pallas_call(functools.partial(update_kernel, n, chunks, layers, count)...]
    pallas_call x3, Pallas kernels: 201 us -> 218 us  [the longest x1 95.7 us: backward_inner(): pl.pallas_call(functools.partial(inner_kernel, n, chunks, tiles, layer),...]
where the time goes in v3:
time: 325 us
  Pallas kernels  324 us (100%)
    pallas_call x1, Pallas kernels, update(): pl.pallas_call(functools.partial(update_kernel, n, chunks, layers, count)...  98.4 us
    pallas_call x1, Pallas kernels, backward_inner(): pl.pallas_call(functools.partial(inner_kernel, n, chunks, tiles, layer),...  95.7 us
    pallas_call x1, Pallas kernels, backward_outer(): pl.pallas_call(functools.partial(outer_kernel, n, chunks, tiles, layer),...  76.2 us
    pallas_call x1, Pallas kernels, forward(): pl.pallas_call(functools.partial(forward_kernel, n, layer, early), grid=(...  45.7 us
    pallas_call x1, Pallas kernels, put(): pl.pallas_call(functools.partial(put_kernel, len(arrays)), in_specs=[pl.B...  8.09 us

profile of v3, /device:TPU:112, one launch (start us, length us, event | category | flops | bytes accessed | tf_op | source)
XLA Modules:
  0.0 325.0 jit_solution(15512445941749371456)
XLA Ops:
  0.6 45.7 %forward.1 = (bf16[640,4096]{1,0:T(8,128)(2,1)}, bf16[4096,640]{1,0:T(8,128)(2,1)}, bf16[640,4096]{1,0:T(8,128)(2,1)}, bf16[640,4096]{1,0:T(8,128)(2,1)}, bf16[6...) custom-call(bf16[4096,640]{1,0:T(8,128)(2,1)} %bitcast.4, ...), custom_call_target="tpu_custom_call" | custom-call | tf_op jit(solution)/shard_map/forward/pallas_call | solution.py:152
  46.3 95.7 %backward_inner.1 = (bf16[2,2,160,512]{3,2,1,0:T(8,128)(2,1)}, bf16[2,128,640]{2,1,0:T(8,128)(2,1)}, f32[2,8,128]{2,1,0:T(8,128)}, bf16[4,2,240,512]{3,2,1,0:T(8...) custom-call(bf16[640,4096]{1,0:T(8,128)(2,1)} %get-tuple-element.36.refs_0_, ...), custom_call_target="tpu_custom_call" | custom-call | tf_op jit(solution)/shard_map/backward_inner/pallas_call | solution.py:570
  142.1 76.2 %backward_outer.1 = (bf16[4,2,160,512]{3,2,1,0:T(8,128)(2,1)}, bf16[4,128,640]{2,1,0:T(8,128)(2,1)}, f32[4,8,128]{2,1,0:T(8,128)}) custom-call(bf16[640,4096]{1,0:T(8,128)(2,1)} %get-tuple-element.43.refs_0_, f32[3,4096,512]{2,1,0:T(8,128)} %get-tuple-element.44.refs_1_, f32[3,4096,512]{2,1,0:T(8,128)} %get-tuple-element.45.refs_2_, ...), custom_call_target="tpu_custom_call" | custom-call | tf_op jit(solution)/shard_map/backward_outer/pallas_call | solution.py:613
  218.3 98.4 %update.1 = (bf16[2,640,1536]{2,1,0:T(8,128)(2,1)S(1)}, bf16[2,640,1536]{2,1,0:T(8,128)(2,1)S(1)}, bf16[2,1536,640]{2,1,0:T(8,128)(2,1)S(1)}, f32[2,160,1536]{2,...) custom-call(bf16[2,2,160,512]{3,2,1,0:T(8,128)(2,1)} %get-tuple-elem, ...), custom_call_target="tpu_custom_call" | custom-call | tf_op jit(solution)/shard_map/update/pallas_call | solution.py:817
  316.7 8.1 %put.1 = (bf16[2,640,1536]{2,1,0:T(8,128)(2,1)}, bf16[2,640,1536]{2,1,0:T(8,128)(2,1)}, bf16[2,1536,640]{2,1,0:T(8,128)(2,1)}, f32[2,160,1536]{2,1,0:T(8,128)}, ...) custom-call(bf16[2,640,1536]{2,1,0:T(8,128)(2,1)S(1)} %get-tuple-ele, ...), custom_call_target="tpu_custom_call" | custom-call | tf_op jit(solution)/shard_map/put/pallas_call | solution.py:855

commit v4 on v3

--- a/solution.py
+++ b/solution.py
@@ -39,7 +39,10 @@
     barrier = pltpu.get_barrier_semaphore()
     for peer in peers:
         pl.semaphore_signal(barrier, inc=1, device_id={AXIS: peer}, device_id_type=MESH)
-    pl.semaphore_wait(barrier, len(peers))
+
+
+def greeted(peers):
+    pl.semaphore_wait(pltpu.get_barrier_semaphore(), len(peers))
 
 
 def fetch(w_refs, layer, n, chunk, buffers, sems):
@@ -88,11 +91,15 @@
                 copy.start()
         me = lax.axis_index(AXIS)
         greet(((me + n - 1) % n, (me + 1) % n))
-        for copy in moments():
-            copy.start()
         for c in range(chunks):
             for copy in weights(c):
                 copy.wait()
+
+    @pl.when(pl.program_id(0) == 1)
+    def _():
+        greeted((0, 1))
+        for copy in moments():
+            copy.start()
 
     def before(p):
         here = slice(p * SUB, (p + 1) * SUB)
@@ -313,13 +320,12 @@
     @pl.when((c == 0) & (t == 0))
     def _():
         greet((ring.left, ring.right))
+
+    @pl.when((c == 0) & (t == 1))
+    def _():
+        greeted((ring.left, ring.right))
         for copy in onward():
             copy.start()
-
-    @pl.when((c == 0) & (t == tiles - 1))
-    def _():
-        for copy in onward():
-            copy.wait()
 
     def weights(chunk, slot):
         return fetch(w_refs, layer, n, chunk, [now.at[slot] for now in (wg_now, wu_now, wd_now)], w_sem.at[slot])
@@ -393,6 +399,11 @@
     @pl.when((c > 0) & (t == tiles - 1))
     def _():
         end(c - 1)
+
+    @pl.when((c == 1) & (t == 0))
+    def _():
+        for copy in onward():
+            copy.wait()
 
     @pl.when((c == 1) & (t == tiles - 1))
     def _():
@@ -442,6 +453,7 @@
         carried.start()
         whole.start()
         greet((ring.left, ring.right))
+        greeted((ring.left, ring.right))
         carried.wait()
         ring.start(0, blocks.at[0])
 
@@ -681,9 +693,9 @@
         done += count_here
     for copy in sum_loads:
         copy.start()
-    for load in loads:
-        for copy in load:
-            copy.start()
+    at_once = layers - 1
+    for copy in loads[at_once]:
+        copy.start()
     own = w_in[0].shape[2] // n
     other_loads = [
         pltpu.make_async_copy(src, dst, early_sem.at[i])
@@ -695,10 +707,9 @@
             other_loads.append(
                 pltpu.make_async_copy(w_in[k].at[layers - 1, :, there], w_early.at[k, :, pl.ds(o * LANES, LANES)], w_sem.at[k, o])
             )
-    for copy in other_loads:
-        copy.start()
     peers = [(me + i) % n for i in range(1, n)]
     greet(peers)
+    greeted(peers)
     for copy in sum_loads:
         copy.wait()
 
@@ -715,6 +726,12 @@
     ]
     for share in shares:
         share.start()
+    for i, load in enumerate(loads):
+        if i != at_once:
+            for copy in load:
+                copy.start()
+    for copy in other_loads:
+        copy.start()
     for share in shares:
         share.wait()
     for i in range(n - 1):

time: 325 us -> 321 us (0.988)
  Pallas kernels: 324 us -> 320 us
    pallas_call x1, Pallas kernels: 98.4 us -> 94.1 us  [update(): pl.pallas_call(functools.partial(update_kernel, n, chunks, layers, count)...]
where the time goes in v4:
time: 321 us
  Pallas kernels  320 us (100%)
    pallas_call x1, Pallas kernels, backward_inner(): pl.pallas_call(functools.partial(inner_kernel, n, chunks, tiles, layer),...  95.5 us
    pallas_call x1, Pallas kernels, update(): pl.pallas_call(functools.partial(update_kernel, n, chunks, layers, count)...  94.1 us
    pallas_call x1, Pallas kernels, backward_outer(): pl.pallas_call(functools.partial(outer_kernel, n, chunks, tiles, layer),...  76.4 us
    pallas_call x1, Pallas kernels, forward(): pl.pallas_call(functools.partial(forward_kernel, n, layer, early), grid=(...  45.9 us
    pallas_call x1, Pallas kernels, put(): pl.pallas_call(functools.partial(put_kernel, len(arrays)), in_specs=[pl.B...  8.09 us

profile of v4, /device:TPU:112, one launch (start us, length us, event | category | flops | bytes accessed | tf_op | source)
XLA Modules:
  0.0 320.8 jit_solution(6214089353168996574)
XLA Ops:
  0.6 45.9 %forward.1 = (bf16[640,4096]{1,0:T(8,128)(2,1)}, bf16[4096,640]{1,0:T(8,128)(2,1)}, bf16[640,4096]{1,0:T(8,128)(2,1)}, bf16[640,4096]{1,0:T(8,128)(2,1)}, bf16[6...) custom-call(bf16[4096,640]{1,0:T(8,128)(2,1)} %bitcast.4, ...), custom_call_target="tpu_custom_call" | custom-call | tf_op jit(solution)/shard_map/forward/pallas_call | solution.py:159
  46.6 95.5 %backward_inner.1 = (bf16[2,2,160,512]{3,2,1,0:T(8,128)(2,1)}, bf16[2,128,640]{2,1,0:T(8,128)(2,1)}, f32[2,8,128]{2,1,0:T(8,128)}, bf16[4,2,240,512]{3,2,1,0:T(8...) custom-call(bf16[640,4096]{1,0:T(8,128)(2,1)} %get-tuple-element.36.refs_0_, ...), custom_call_target="tpu_custom_call" | custom-call | tf_op jit(solution)/shard_map/backward_inner/pallas_call | solution.py:582
  142.1 76.4 %backward_outer.1 = (bf16[4,2,160,512]{3,2,1,0:T(8,128)(2,1)}, bf16[4,128,640]{2,1,0:T(8,128)(2,1)}, f32[4,8,128]{2,1,0:T(8,128)}) custom-call(bf16[640,4096]{1,0:T(8,128)(2,1)} %get-tuple-element.43.refs_0_, f32[3,4096,512]{2,1,0:T(8,128)} %get-tuple-element.44.refs_1_, f32[3,4096,512]{2,1,0:T(8,128)} %get-tuple-element.45.refs_2_, ...), custom_call_target="tpu_custom_call" | custom-call | tf_op jit(solution)/shard_map/backward_outer/pallas_call | solution.py:625
  218.5 94.1 %update.1 = (bf16[2,640,1536]{2,1,0:T(8,128)(2,1)S(1)}, bf16[2,640,1536]{2,1,0:T(8,128)(2,1)S(1)}, bf16[2,1536,640]{2,1,0:T(8,128)(2,1)S(1)}, f32[2,160,1536]{2,...) custom-call(bf16[2,2,160,512]{3,2,1,0:T(8,128)(2,1)} %get-tuple-elem, ...), custom_call_target="tpu_custom_call" | custom-call | tf_op jit(solution)/shard_map/update/pallas_call | solution.py:834
  312.6 8.1 %put.1 = (bf16[2,640,1536]{2,1,0:T(8,128)(2,1)}, bf16[2,640,1536]{2,1,0:T(8,128)(2,1)}, bf16[2,1536,640]{2,1,0:T(8,128)(2,1)}, f32[2,160,1536]{2,1,0:T(8,128)}, ...) custom-call(bf16[2,640,1536]{2,1,0:T(8,128)(2,1)S(1)} %get-tuple-ele, ...), custom_call_target="tpu_custom_call" | custom-call | tf_op jit(solution)/shard_map/put/pallas_call | solution.py:872

commit v5 on v4

--- a/solution.py
+++ b/solution.py
@@ -527,8 +527,9 @@
     @pl.when(t == tiles - 1)
     def _():
         pack(here, n, 2, acc)
+        ring.start(i, here, (2,))
         pack(here, n, 0, acc_g)
-        ring.start(i, here, (2, 0))
+        ring.start(i, here, (0,))
 
     @pl.when(t == tiles)
     def _():

time: 321 us -> 319 us (level)
  no operation moved by 1% of the time
where the time goes in v5:
time: 319 us
  Pallas kernels  318 us (100%)
    pallas_call x1, Pallas kernels, backward_inner(): pl.pallas_call(functools.partial(inner_kernel, n, chunks, tiles, layer),...  95.5 us
    pallas_call x1, Pallas kernels, update(): pl.pallas_call(functools.partial(update_kernel, n, chunks, layers, count)...  92 us
    pallas_call x1, Pallas kernels, backward_outer(): pl.pallas_call(functools.partial(outer_kernel, n, chunks, tiles, layer),...  76.9 us
    pallas_call x1, Pallas kernels, forward(): pl.pallas_call(functools.partial(forward_kernel, n, layer, early), grid=(...  45.9 us
    pallas_call x1, Pallas kernels, put(): pl.pallas_call(functools.partial(put_kernel, len(arrays)), in_specs=[pl.B...  8.09 us

profile of v5, /device:TPU:112, one launch (start us, length us, event | category | flops | bytes accessed | tf_op | source)
XLA Modules:
  0.0 319.3 jit_solution(14286071607917115990)
XLA Ops:
  0.6 45.9 %forward.1 = (bf16[640,4096]{1,0:T(8,128)(2,1)}, bf16[4096,640]{1,0:T(8,128)(2,1)}, bf16[640,4096]{1,0:T(8,128)(2,1)}, bf16[640,4096]{1,0:T(8,128)(2,1)}, bf16[6...) custom-call(bf16[4096,640]{1,0:T(8,128)(2,1)} %bitcast.4, ...), custom_call_target="tpu_custom_call" | custom-call | tf_op jit(solution)/shard_map/forward/pallas_call | solution.py:159
  46.6 95.5 %backward_inner.1 = (bf16[2,2,160,512]{3,2,1,0:T(8,128)(2,1)}, bf16[2,128,640]{2,1,0:T(8,128)(2,1)}, f32[2,8,128]{2,1,0:T(8,128)}, bf16[4,2,240,512]{3,2,1,0:T(8...) custom-call(bf16[640,4096]{1,0:T(8,128)(2,1)} %get-tuple-element.36.refs_0_, ...), custom_call_target="tpu_custom_call" | custom-call | tf_op jit(solution)/shard_map/backward_inner/pallas_call | solution.py:583
  142.1 76.9 %backward_outer.1 = (bf16[4,2,160,512]{3,2,1,0:T(8,128)(2,1)}, bf16[4,128,640]{2,1,0:T(8,128)(2,1)}, f32[4,8,128]{2,1,0:T(8,128)}) custom-call(bf16[640,4096]{1,0:T(8,128)(2,1)} %get-tuple-element.43.refs_0_, f32[3,4096,512]{2,1,0:T(8,128)} %get-tuple-element.44.refs_1_, f32[3,4096,512]{2,1,0:T(8,128)} %get-tuple-element.45.refs_2_, ...), custom_call_target="tpu_custom_call" | custom-call | tf_op jit(solution)/shard_map/backward_outer/pallas_call | solution.py:626
  219.0 92.0 %update.1 = (bf16[2,640,1536]{2,1,0:T(8,128)(2,1)S(1)}, bf16[2,640,1536]{2,1,0:T(8,128)(2,1)S(1)}, bf16[2,1536,640]{2,1,0:T(8,128)(2,1)S(1)}, f32[2,160,1536]{2,...) custom-call(bf16[2,2,160,512]{3,2,1,0:T(8,128)(2,1)} %get-tuple-elem, ...), custom_call_target="tpu_custom_call" | custom-call | tf_op jit(solution)/shard_map/update/pallas_call | solution.py:835
  311.0 8.1 %put.1 = (bf16[2,640,1536]{2,1,0:T(8,128)(2,1)}, bf16[2,640,1536]{2,1,0:T(8,128)(2,1)}, bf16[2,1536,640]{2,1,0:T(8,128)(2,1)}, f32[2,160,1536]{2,1,0:T(8,128)}, ...) custom-call(bf16[2,640,1536]{2,1,0:T(8,128)(2,1)S(1)} %get-tuple-ele, ...), custom_call_target="tpu_custom_call" | custom-call | tf_op jit(solution)/shard_map/put/pallas_call | solution.py:873
